TPU v7x, 16 devices: a 4x2x1 block of a 4x4x8 slice. The times are simulated.
16 devices in a mesh: dp: 2 (over y, z), tp: 8 (over x, core).
Axes of the slice: x: 4, y: 2, z: 1, core: 2. Of those that a mesh axis runs over, the one named last changes fastest.
The devices are a block of a 4x4x8 slice.
Arguments:
- hidden: bfloat16 [128, 5120], P('dp'), parts along dimension 0
- cache_len: int32 [128], P('dp'), parts along dimension 0
- lin_state: float32 [128, 40, 128, 128], P('dp', 'tp'), parts along dimension 0
- k_cache: bfloat16 [128, 8, 512, 128], P('dp', 'tp'), parts along dimension 0
- v_cache: bfloat16 [128, 8, 512, 128], P('dp', 'tp'), parts along dimension 0
- norm_first: float32 [5120], replicated
- w_qkv: bfloat16 [5120, 3, 40, 128], P(None, None, 'tp')
- w_gate: bfloat16 [5120, 40, 128], P(None, 'tp')
- slopes: float32 [40], P('tp')
- out_norm: float32 [40, 128], P('tp')
- w_out_lin: bfloat16 [40, 128, 5120], P('tp')
- norm_second: float32 [5120], replicated
- w_attn: bfloat16 [5120, 8, 7, 128], P(None, 'tp')
- w_out_attn: bfloat16 [40, 128, 5120], P('tp')
- mix_alpha: float32 [2], replicated
- mix_beta: float32 [2], replicated
Outputs:
- output 1: bfloat16 [128, 5120], P('dp'), parts along dimension 0
- output 2: float32 [128, 40, 128, 128], P('dp', 'tp'), parts along dimension 0
- output 3: bfloat16 [128, 8, 512, 128], P('dp', 'tp'), parts along dimension 0
- output 4: bfloat16 [128, 8, 512, 128], P('dp', 'tp'), parts along dimension 0
There are 2 independent parts. A program takes and returns all parts, laid end to end along the dimension named above; an argument that names none is the same for every part.
All inputs are finite; a program needn't handle non-finite values.
Results may differ from a plain program's by a relative error of at most 0.0114051.
Values sent between devices are 32-bit elements.
A program may use at most 768 MiB of HBM per device.

v0:
```python
import jax
import jax.numpy as jnp
from jax import lax
from jax.sharding import PartitionSpec as P

EPS = 1e-5
ROPE_BASE = 10000000.0


def rms_scale(values, gain_vec):
    wide_vals = values.astype(jnp.float32)
    return wide_vals * lax.rsqrt(jnp.mean(wide_vals * wide_vals, axis=-1, keepdims=True) + EPS) * gain_vec


def rotary(values, positions):
    rot_dim = values.shape[-1] // 2
    half_dim = rot_dim // 2
    inv_freq = ROPE_BASE ** (-2.0 * jnp.arange(half_dim, dtype=jnp.float32) / rot_dim)
    angles = positions.astype(jnp.float32)[:, None] * inv_freq[None, :]
    cosine = jnp.cos(angles)[:, None, None, :]
    sine_val = jnp.sin(angles)[:, None, None, :]
    rot_first = values[..., :half_dim]
    rot_second = values[..., half_dim:rot_dim]
    return jnp.concatenate([rot_first * cosine - rot_second * sine_val,
                            rot_second * cosine + rot_first * sine_val,
                            values[..., rot_dim:]], axis=-1)


def solution(mesh):
    tp_size = mesh.shape['tp']
    row_spec = P('dp', None)
    cache_spec = P('dp', 'tp', None, None)
    in_specs = (row_spec, P('dp'), cache_spec, cache_spec, cache_spec, P(None), P(None, None, 'tp', None),
                P(None, 'tp', None), P('tp'), P('tp', None), P('tp', None, None), P(None),
                P(None, 'tp', None, None), P('tp', None, None), P(None), P(None))
    out_specs = (row_spec, cache_spec, cache_spec, cache_spec)

    def local_step(hidden, cache_len, lin_state, k_cache, v_cache, norm_first, w_qkv, w_gate, slopes, out_norm,
                   w_out_lin, norm_second, w_attn, w_out_attn, mix_alpha, mix_beta):
        head_dim = k_cache.shape[3]
        full_width = w_out_lin.shape[0] * head_dim * tp_size
        kv_local = w_attn.shape[1]
        group_size = w_attn.shape[2] - 2
        h_first = rms_scale(hidden, norm_first).astype(jnp.bfloat16)
        proj_lin = jax.nn.silu(jnp.einsum('bd,dchk->bchk', h_first, w_qkv, preferred_element_type=jnp.float32)).astype(jnp.bfloat16)
        decay_rate = jnp.exp(-slopes)[None, :, None, None]
        state_out = decay_rate * lin_state + jnp.einsum('bhk,bhv->bhkv', proj_lin[:, 1], proj_lin[:, 2], preferred_element_type=jnp.float32)
        lin_attn = jnp.einsum('bhk,bhkv->bhv', proj_lin[:, 0].astype(jnp.float32), state_out, precision=lax.Precision.HIGHEST)
        sq_sum = lax.psum(jnp.sum(lin_attn * lin_attn, axis=(1, 2)), 'tp')
        inv_rms = lax.rsqrt(sq_sum / full_width + EPS)[:, None, None]
        gate_val = jax.nn.sigmoid(jnp.einsum('bd,dhk->bhk', h_first, w_gate, preferred_element_type=jnp.float32))
        gated_out = (lin_attn * inv_rms * out_norm * gate_val).astype(jnp.bfloat16)
        lin_part = jnp.einsum('bhk,hkd->bd', gated_out, w_out_lin, preferred_element_type=jnp.float32)
        lin_out = lax.psum(lin_part, 'tp')
        mid_hidden = (mix_alpha[0] * h_first.astype(jnp.float32) + mix_beta[0] * lin_out).astype(jnp.bfloat16)
        h_second = rms_scale(mid_hidden, norm_second).astype(jnp.bfloat16)
        proj_attn = jnp.einsum('bd,dkjc->bkjc', h_second, w_attn, preferred_element_type=jnp.float32)
        turned = rotary(proj_attn[:, :, :group_size + 1], cache_len).astype(jnp.bfloat16)
        key_new = turned[:, :, group_size][:, :, None, :]
        value_new = proj_attn[:, :, group_size + 1].astype(jnp.bfloat16)[:, :, None, :]
        positions = jnp.arange(k_cache.shape[2], dtype=jnp.int32)
        write_mask = (positions[None, :] == cache_len[:, None])[:, None, :, None]
        k_out = jnp.where(write_mask, key_new, k_cache)
        v_out = jnp.where(write_mask, value_new, v_cache)
        scores = jnp.einsum('bkgc,bktc->bkgt', turned[:, :, :group_size], k_out, preferred_element_type=jnp.float32) * head_dim ** -0.5
        valid_mask = (positions[None, :] <= cache_len[:, None])[:, None, None, :]
        probs_bf = jax.nn.softmax(jnp.where(valid_mask, scores, -jnp.inf), axis=-1).astype(jnp.bfloat16)
        attn_rows = jnp.einsum('bkgt,bktc->bkgc', probs_bf, v_out, preferred_element_type=jnp.float32).astype(jnp.bfloat16)
        w_out_grouped = w_out_attn.reshape(kv_local, group_size, head_dim, w_out_attn.shape[2])
        attn_part = jnp.einsum('bkgc,kgcd->bd', attn_rows, w_out_grouped, preferred_element_type=jnp.float32)
        attn_out = lax.psum(attn_part, 'tp')
        hidden_out = (mix_alpha[1] * h_second.astype(jnp.float32) + mix_beta[1] * attn_out).astype(jnp.bfloat16)
        return hidden_out, state_out, k_out, v_out

    return jax.shard_map(local_step, mesh=mesh, in_specs=in_specs, out_specs=out_specs, check_vma=False)
```

profile of v0, /device:TPU:113, one launch (start us, length us, event | category | flops | bytes accessed | tf_op | source)
XLA Modules:
  0.0 213.5 jit_solution(8855164971802041600)
XLA Ops:
  7.2 0.7 negate_exponential_fusion
  7.9 1.3 fusion.9
  9.2 10.4 %multiply_convert_fusion = bf16[64,3,5,128]{3,0,2,1:T(8,128)(2,1)S(1)} fusion(bf16[5120,3,5,128]{3,0,2,1:T(8,128)(2,1)} %param.22, bf16[64,5120]{1,0:T(8,128)(2,1)} %param.16, f32[5120]{0:T(1024)} %param.21, f32[64]{0:T(128)S(1)} %add_rsqrt_fusion.2), kind=kOutput, calls=%fused_computation.41 | convolution fusion | flops 1260216320 | bytes 20582656 | tf_op jit(solution)/shard_map/bd,dchk->bchk/dot_general | solution.py:45
  19.9 9.5 %multiply_add_fusion = f32[64,5,128,128]{3,2,1,0:T(8,128)S(1)} fusion(f32[64,5,128,128]{3,2,1,0:T(8,128)} %param.18, f32[64,5,128]{2,1,0:T(8,128)S(1)} %copy.21, f32[64,5,128]{2,1,0:T(8,128)S(1)} %copy.20, f32[5]{0:T(128)S(1)} %negate_exponential_fusion), kind=kLoop, calls=%fused_computation.1 | loop fusion | flops 15728640 | bytes 42270740 | tf_op jit(solution)/shard_map/add | solution.py:47
  29.4 9.7 %fusion.41 = f32[64,5,1,128]{3,2,1,0:T(1,128)S(1)} fusion(f32[64,5,128,128]{3,2,1,0:T(8,128)S(1)} %multiply_add_fusion, bf16[64,5,128,1]{2,0,1,3:T(8,128)(2,1)S(1)} %get-tuple-element.8), kind=kOutput, calls=%fused_computation.49 | convolution fusion | flops 62914560 | bytes 21217280 | tf_op jit(solution)/shard_map/bhk,bhkv->bhv/dot_general | solution.py:48
  39.3 13.6 %psum.21 = f32[64]{0:T(128)S(1)} all-reduce(f32[64]{0:T(128)S(1)} %fusion.38), channel_id=1, replica_groups=mesh['dp'=2,'tp'=8] {'tp'}, use_global_device_ids=true, to_apply=%region_2.3 | all-reduce | flops 64 | bytes 512 | tf_op jit(solution)/shard_map/psum | solution.py:49
  53.0 8.3 %convolution_bitcast_fusion.1 = f32[64,5120]{1,0:T(8,128)} fusion(bf16[5,128,5120]{2,1,0:T(8,128)(2,1)} %param.26, bf16[5120,5,128]{2,0,1:T(8,128)(2,1)} %param.23, f32[64,5,1,128]{3,2,1,0:T(1,128)S(1)} %fusion.41, f32[5,128]{1,0:T(8,128)S(1)} %copy-done.5, f32[64]{0:T(128)S(1)} %add_rsqrt_fusion.1, bf16[64,5120]{1,0:T(8,128)(2,1)S(1)} %copy-done.2, ...), kind=kOutput, calls=%fused_computation.11 | convolution fusion | flops 840458240 | bytes 15260672 | tf_op jit(solution)/shard_map/bhk,hkd->bd/dot_general | solution.py:53
  61.3 0.2 all-reduce.5.cloned.1.call-start
  61.6 0.7 fusion.54
  62.3 0.6 fusion.55
  63.0 0.2 multiply_cosine_fusion
  63.2 53.2 %all-reduce.3.cloned.1.call-done = f32[64,5120]{1,0:T(8,128)} async-done(((f32[64,5120]{1,0:T(8,128)}), f32[64,5120]{1,0:T(8,128)}) %all-reduce.3.cloned.1.call-update) | async-done | bytes 1310736 | tf_op jit(solution)/shard_map/psum | solution.py:54
  116.3 3.1 %fusion.12 = (f32[64]{0:T(128)S(1)}, bf16[64,5120]{1,0:T(8,128)(2,1)S(1)}) fusion(f32[64,5120]{1,0:T(8,128)} %all-reduce.3.cloned.1.call-done, f32[]{:T(128)} %bitcast.2, f32[5120]{0:T(1024)S(1)} %copy-done.3, f32[64]{0:T(128)S(1)} %add_rsqrt_fusion.2, bf16[64,5120]{1,0:T(8,128)(2,1)S(1)} %copy-done.2, f32[]{:T(128)} %bitcast.1), kind=kLoop, calls=%fused_computation.21 | loop fusion | flops 3932096 | bytes 2642440 | tf_op jit(solution)/shard_map/reduce_sum | solution.py:12
  119.5 5.3 %fusion.56 = (bf16[64,1,7,128]{3,0,2,1:T(8,128)(2,1)S(1)}, f32[64,1,7,128]{3,0,2,1:T(8,128)S(1)}) fusion(bf16[5120,1,7,128]{3,0,2,1:T(8,128)(2,1)} %param.28, f32[5120]{0:T(1024)S(1)} %copy-done.4, f32[64]{0:T(128)S(1)} %add_rsqrt_fusion, bf16[64,5120]{1,0:T(8,128)(2,1)S(1)} %get-tuple-element.5), kind=kOutput, calls=%fused_computation.77 | convolution fusion | flops 588570624 | bytes 10195200 | tf_op jit(solution)/shard_map/bd,dkjc->bkjc/dot_general | solution.py:57
  124.9 0.1 subtract_convert_fusion
  125.1 0.1 pad_maximum_fusion
  125.3 9.5 %broadcast_select_fusion.1 = (bf16[64,1,512,128]{3,2,1,0:T(8,128)(2,1)S(1)}, bf16[64,1,512,128]{3,2,1,0:T(8,128)(2,1)}) fusion(bf16[64,1,512,128]{3,2,1,0:T(8,128)(2,1)} %param.19, pred[64,512]{1,0:T(8,128)(4,1)S(1)} %get-tuple-element.20, bf16[64,128]{1,0:T(8,128)(2,1)S(1)} %get-tuple-element.24, bf16[64,1,512,128]{3,2,1,0:T(8,128)(2,1)} %param.20, ...), kind=kLoop, calls=%fused_computation.9 | loop fusion | flops 8388608 | bytes 33619968 | tf_op jit(solution)/shard_map/jit(_where)/select_n | solution.py:63
  134.8 2.3 %fusion.18 = f32[64,5,512]{2,1,0:T(8,128)S(1)} fusion(bf16[64,1,512,128]{3,2,1,0:T(8,128)(2,1)S(1)} %get-tuple-element.11, pred[64,512]{1,0:T(8,128)(4,1)S(1)} %get-tuple-element.19, bf16[64,5,128]{2,0,1:T(8,128)(2,1)S(1)} %slice_bitcast_fusion), kind=kOutput, calls=%fused_computation.27 | convolution fusion | flops 42270720 | bytes 9158656 | tf_op jit(solution)/shard_map/bkgc,bktc->bkgt/dot_general | solution.py:65
  137.1 1.1 copy-done.1
  138.2 0.3 fusion.57
  138.5 4.6 %fusion.3 = bf16[64,5,128]{2,1,0:T(8,128)(2,1)S(1)} fusion(bf16[64,1,512,128]{3,2,1,0:T(8,128)(2,1)} %get-tuple-element.12, f32[64,5]{1,0:T(8,128)S(1)} %fusion.57, f32[64,5,512]{2,1,0:T(8,128)S(1)} %fusion.18), kind=kOutput, calls=%fused_computation.4 | convolution fusion | flops 42435392 | bytes 9127168 | tf_op jit(solution)/shard_map/bkgt,bktc->bkgc/dot_general | solution.py:68
  143.1 5.2 %convolution_bitcast_fusion = f32[64,5120]{1,0:T(8,128)} fusion(bf16[5,128,5120]{2,1,0:T(8,128)(2,1)} %param.29, bf16[64,5,128]{2,1,0:T(8,128)(2,1)S(1)} %fusion.3), kind=kOutput, calls=%fused_computation.10 | convolution fusion | flops 419430400 | bytes 7946240 | tf_op jit(solution)/shard_map/bkgc,kgcd->bd/dot_general | solution.py:70
  148.4 54.5 %all-reduce.5.cloned.1.call-done = f32[64,5120]{1,0:T(8,128)} async-done(((f32[64,5120]{1,0:T(8,128)}), f32[64,5120]{1,0:T(8,128)}) %all-reduce.5.cloned.1.call-update) | async-done | bytes 1310736 | tf_op jit(solution)/shard_map/psum | solution.py:71
  203.0 3.7 %add_convert_fusion = bf16[64,5120]{1,0:T(8,128)(2,1)} fusion(f32[64,5120]{1,0:T(8,128)} %all-reduce.5.cloned.1.call-done, f32[]{:T(128)} %bitcast.12, f32[]{:T(128)} %bitcast, f32[5120]{0:T(1024)S(1)} %copy-done.4, f32[64]{0:T(128)S(1)} %add_rsqrt_fusion, bf16[64,5120]{1,0:T(8,128)(2,1)S(1)} %get-tuple-element.5), kind=kLoop, calls=%fused_computation.24 | loop fusion | flops 2949120 | bytes 2642184 | tf_op jit(solution)/shard_map/convert_element_type | solution.py:72
  (33 shorter events, 0.9 us)
Async XLA Ops:
  7.2 109.2 %all-reduce.3.cloned.1.call-start = ((), (), s32[]{:S(2)}) async-start(), calls=%async_computation | async-start | bytes 2621440 | tf_op jit(solution)/shard_map/psum | solution.py:54
  29.4 9.8 %copy-start = (f32[64,5,128,128]{3,2,1,0:T(8,128)}, f32[64,5,128,128]{3,2,1,0:T(8,128)S(1)}, u32[]{:S(2)}) copy-start(f32[64,5,128,128]{3,2,1,0:T(8,128)S(1)} %multiply_add_fusion) | copy-start | bytes 62914564
  29.4 23.5 %copy-start.2 = (bf16[64,5120]{1,0:T(8,128)(2,1)S(1)}, bf16[64,5120]{1,0:T(8,128)(2,1)}, u32[]{:S(2)}) copy-start(bf16[64,5120]{1,0:T(8,128)(2,1)} %param.16) | copy-start | bytes 1966084
  29.4 23.5 %copy-start.3 = (f32[5120]{0:T(1024)S(1)}, f32[5120]{0:T(1024)}, u32[]{:S(2)}) copy-start(f32[5120]{0:T(1024)} %param.21) | copy-start | bytes 61444
  29.4 23.5 %copy-start.5 = (f32[5,128]{1,0:T(8,128)S(1)}, f32[5,128]{1,0:T(8,128)}, u32[]{:S(2)}) copy-start(f32[5,128]{1,0:T(8,128)} %param.25) | copy-start | bytes 7684
  52.9 8.7 %copy-start.8 = (s32[64]{0:T(128)S(1)}, s32[64]{0:T(128)}, u32[]{:S(2)}) copy-start(s32[64]{0:T(128)} %param.17) | copy-start | bytes 772
  52.9 8.7 %copy-start.6 = (f32[2]{0:T(128)S(1)}, f32[2]{0:T(128)}, u32[]{:S(2)}) copy-start(f32[2]{0:T(128)} %param.30) | copy-start | bytes 28
  52.9 9.3 %copy-start.7 = (f32[2]{0:T(128)S(1)}, f32[2]{0:T(128)}, u32[]{:S(2)}) copy-start(f32[2]{0:T(128)} %param.31) | copy-start | bytes 28
  52.9 66.5 %copy-start.4 = (f32[5120]{0:T(1024)S(1)}, f32[5120]{0:T(1024)}, u32[]{:S(2)}) copy-start(f32[5120]{0:T(1024)} %param.27) | copy-start | bytes 61444
  61.3 141.6 %all-reduce.5.cloned.1.call-start = ((), (), s32[]{:S(2)}) async-start(), calls=%async_computation.1 | async-start | bytes 2621440 | tf_op jit(solution)/shard_map/psum | solution.py:71
  134.8 3.4 %copy-start.1 = (bf16[64,1,512,128]{3,2,1,0:T(8,128)(2,1)}, bf16[64,1,512,128]{3,2,1,0:T(8,128)(2,1)S(1)}, u32[]{:S(2)}) copy-start(bf16[64,1,512,128]{3,2,1,0:T(8,128)(2,1)S(1)} %get-tuple-element.11) | copy-start | bytes 25165828
Sparse Core Ops, SparseCore 0:
  61.4 54.8 all-reduce.2
  148.6 54.3 all-reduce.4
where the time goes:
time: 216 us; the launch traced here: 214 us
  waiting for transfers between devices  108 us (50%)
  matrix products  45.9 us (21%)
  other arithmetic  28.9 us (13%)
  between operations  14.3 us (7%)
  blocking collectives  13.6 us (6%)
  local copies, waits for them, and re-layouts  2.73 us (1%)
    psum x1, waiting for transfers between devices, local_step(): attn_out = lax.psum(attn_part, 'tp')  54.5 us
    psum x1, waiting for transfers between devices, local_step(): lin_out = lax.psum(lin_part, 'tp')  53.2 us
    psum x1, blocking collectives, local_step(): sq_sum = lax.psum(jnp.sum(lin_attn * lin_attn, axis=(1, 2)), 'tp')  13.6 us
    dot_general x1, matrix products, local_step(): jnp.einsum('bd,dchk->bchk', h_first, w_qkv, preferred_element_type=jnp.fl...  10.4 us
    dot_general x1, matrix products, local_step(): jnp.einsum('bhk,bhkv->bhv', proj_lin[:, 0].astype(jnp.float32), state_out...  9.75 us
    select_n x1, other arithmetic, local_step(): k_out = jnp.where(write_mask, key_new, k_cache)  9.47 us
    add x1, other arithmetic, local_step(): decay_rate * lin_state  9.46 us
    dot_general x1, matrix products, local_step(): jnp.einsum('bhk,hkd->bd', gated_out, w_out_lin, preferred_element_type=jn...  8.31 us
  transfers between devices with their start and end apart: 2, of which 2 were waited for; matrix products, arithmetic and copies ran while one was open for 1% of the time, Pallas kernels for 0%

commit v1 on v0

v1 whole, which is shorter than its diff:
```python
import functools

import jax
import jax.numpy as jnp
from jax import lax
from jax.experimental import pallas as pl
from jax.experimental.pallas import tpu as pltpu
from jax.sharding import PartitionSpec as P

EPS = 1e-5
ROPE_BASE = 10000000.0
MESH = pl.DeviceIdType.MESH
VMEM = pl.BlockSpec(memory_space=pltpu.VMEM)
SMEM = pl.BlockSpec(memory_space=pltpu.SMEM)
HBM = pl.BlockSpec(memory_space=pltpu.HBM)
ROWS = 8
LANES = 128


def lightning_kernel(slopes_ref, hidden_ref, norm_ref, wqkv_ref, wgate_ref, state_ref, onorm_ref, wout_ref,
                     state_out_ref, part_ref, h1_out_ref,
                     h1_ref, sq_ref, kt_ref, qt_ref, v_ref, o_ref):
    head = pl.program_id(0)
    heads = pl.num_programs(0)
    batch, width = hidden_ref.shape

    @pl.when(head == 0)
    def _():
        x = hidden_ref[...].astype(jnp.float32)
        h1 = x * lax.rsqrt(jnp.mean(x * x, axis=-1, keepdims=True) + EPS) * norm_ref[...]
        h1 = h1.astype(jnp.bfloat16)
        h1_ref[...] = h1
        h1_out_ref[...] = h1.astype(jnp.float32).reshape(h1_out_ref.shape)
        sq_ref[...] = jnp.zeros_like(sq_ref)

    def project(w):
        return jnp.dot(h1_ref[...], w, preferred_element_type=jnp.float32)

    def silu(x):
        return (x * jax.nn.sigmoid(x)).astype(jnp.bfloat16).astype(jnp.float32)

    q = silu(project(wqkv_ref[0, 0]))
    k = silu(project(wqkv_ref[1, 0]))
    v = silu(project(wqkv_ref[2, 0]))
    gate = jax.nn.sigmoid(project(wgate_ref[0]))
    v_ref[...] = v
    kt = k.T
    qt = q.T
    for i in range(batch // ROWS):
        kt_ref[i] = kt[:, i * ROWS:(i + 1) * ROWS]
        qt_ref[i] = qt[:, i * ROWS:(i + 1) * ROWS]
    decay = jnp.exp(-jnp.full((1, LANES), slopes_ref[head], jnp.float32))

    def block(i, _):
        kb, qb = kt_ref[i], qt_ref[i]
        base = pl.multiple_of(i * ROWS, ROWS)
        vb = v_ref[pl.ds(base, ROWS), :]
        outs = []
        for r in range(ROWS):
            new = decay * state_ref[base + r, 0] + kb[:, r:r + 1] * vb[r:r + 1, :]
            state_out_ref[base + r, 0] = new
            outs.append(jnp.sum(qb[:, r:r + 1] * new, axis=0, keepdims=True))
        o_ref[pl.ds(base, ROWS), :] = jnp.concatenate(outs, axis=0)
        return 0

    lax.fori_loop(0, batch // ROWS, block, 0)
    o = o_ref[...]
    sq_ref[...] += jnp.broadcast_to(jnp.sum(o * o, axis=1, keepdims=True), sq_ref.shape)
    gated = (o * onorm_ref[0] * gate).astype(jnp.bfloat16)
    tile = 1024
    for c in range(width // tile):
        cols = pl.ds(c * tile, tile)
        piece = jnp.dot(gated, wout_ref[0, :, cols], preferred_element_type=jnp.float32)
        piece = piece.reshape(batch // ROWS, ROWS, tile)

        @pl.when(head == 0)
        def _():
            part_ref[:, :, cols] = piece

        @pl.when(head > 0)
        def _():
            part_ref[:, :, cols] += piece

    @pl.when(head == heads - 1)
    def _():
        part_ref[:, :, pl.ds(width, LANES)] = sq_ref[...].reshape(batch // ROWS, ROWS, LANES)


def lightning(hidden, norm_first, w_qkv, w_gate, lin_state, slopes, out_norm, w_out_lin):
    batch, width = hidden.shape
    heads, dim = out_norm.shape
    blocks = batch // ROWS
    return pl.pallas_call(
        lightning_kernel,
        grid=(heads,),
        out_shape=(jax.ShapeDtypeStruct(lin_state.shape, jnp.float32),
                   jax.ShapeDtypeStruct((blocks, ROWS, width + LANES), jnp.float32),
                   jax.ShapeDtypeStruct((blocks, ROWS, width), jnp.float32)),
        in_specs=[
            SMEM,
            pl.BlockSpec((batch, width), lambda h: (0, 0)),
            pl.BlockSpec((1, width), lambda h: (0, 0)),
            pl.BlockSpec((3, 1, width, dim), lambda h: (0, h, 0, 0)),
            pl.BlockSpec((1, width, dim), lambda h: (h, 0, 0)),
            pl.BlockSpec((batch, 1, dim, dim), lambda h: (0, h, 0, 0)),
            pl.BlockSpec((1, 1, dim), lambda h: (h, 0, 0)),
            pl.BlockSpec((1, dim, width), lambda h: (h, 0, 0)),
        ],
        out_specs=(
            pl.BlockSpec((batch, 1, dim, dim), lambda h: (0, h, 0, 0)),
            pl.BlockSpec((blocks, ROWS, width + LANES), lambda h: (0, 0, 0)),
            pl.BlockSpec((blocks, ROWS, width), lambda h: (0, 0, 0)),
        ),
        scratch_shapes=[
            pltpu.VMEM((batch, width), jnp.bfloat16),
            pltpu.VMEM((batch, LANES), jnp.float32),
            pltpu.VMEM((blocks, dim, ROWS), jnp.float32),
            pltpu.VMEM((blocks, dim, ROWS), jnp.float32),
            pltpu.VMEM((batch, dim), jnp.float32),
            pltpu.VMEM((batch, dim), jnp.float32),
        ],
        compiler_params=pltpu.CompilerParams(vmem_limit_bytes=56 << 20),
        cost_estimate=pl.CostEstimate(flops=2 * batch * width * heads * dim * 5, transcendentals=0,
                                      bytes_accessed=2 * lin_state.size * 4 + 10 * heads * dim * width),
        name="lightning",
    )(slopes, hidden, norm_first.reshape(1, width), w_qkv.transpose(1, 2, 0, 3), w_gate.transpose(1, 0, 2),
      lin_state, out_norm.reshape(heads, 1, dim), w_out_lin)


def reduce_kernel(finish, chips, split, n_extra, part_ref, *refs):
    extra, (all_ref, own_ref), scratch = refs[:n_extra], refs[n_extra:n_extra + 2], refs[n_extra + 2:]
    pair_ref, acc_ref, up_a, up_b, up_c, down_a, down_b, down_c, gather_ref, send_sem, recv_sem = scratch
    width = part_ref.shape[2]
    out_width = gather_ref.shape[2]
    cut = out_width // 2
    me = lax.axis_index("tp")
    chip, core = me // 2, me % 2
    mate = 2 * chip + (1 - core)
    next_chip, prev_chip, far_chip = (chip + 1) % chips, (chip + chips - 1) % chips, (chip + 2) % chips
    up, down = 2 * next_chip + core, 2 * prev_chip + core

    barrier = pltpu.get_barrier_semaphore()
    for peer in (mate, up, down):
        pl.semaphore_signal(barrier, inc=1, device_id={"tp": peer}, device_id_type=MESH)
    pl.semaphore_wait(barrier, 3)

    counter = iter(range(64))

    def copy(src, dst, peer):
        i = next(counter)
        return pltpu.make_async_remote_copy(src_ref=src, dst_ref=dst, send_sem=send_sem.at[i], recv_sem=recv_sem.at[i],
                                            device_id={"tp": peer}, device_id_type=MESH)

    lo, hi = pl.ds(0, split), pl.ds(split, width - split)

    pair = [copy(part_ref.at[2 * t + (1 - core)], pair_ref.at[s], mate)
            for s, t in enumerate((far_chip, next_chip, prev_chip, chip))]
    for c in pair:
        c.start()
    pair[0].wait_recv()
    acc_ref[0] = part_ref[2 * far_chip + core] + pair_ref[0]
    far_up = copy(acc_ref.at[0, :, lo], up_a, up)
    far_down = copy(acc_ref.at[0, :, hi], down_a, down)
    far_up.start()
    far_down.start()
    pair[1].wait_recv()
    acc_ref[1] = part_ref[2 * next_chip + core] + pair_ref[1]
    near_up = copy(acc_ref.at[1, :, hi], up_b, up)
    near_up.start()
    pair[2].wait_recv()
    acc_ref[2] = part_ref[2 * prev_chip + core] + pair_ref[2]
    near_down = copy(acc_ref.at[2, :, lo], down_b, down)
    near_down.start()
    far_up.wait_recv()
    acc_ref[1, :, lo] += up_a[...]
    sum_up = copy(acc_ref.at[1, :, lo], up_c, up)
    sum_up.start()
    far_down.wait_recv()
    acc_ref[2, :, hi] += down_a[...]
    sum_down = copy(acc_ref.at[2, :, hi], down_c, down)
    sum_down.start()
    pair[3].wait_recv()
    acc_ref[3] = part_ref[me] + pair_ref[3]
    near_up.wait_recv()
    acc_ref[3, :, hi] += up_b[...]
    near_down.wait_recv()
    acc_ref[3, :, lo] += down_b[...]
    sum_up.wait_recv()
    acc_ref[3, :, lo] += up_c[...]
    sum_down.wait_recv()
    acc_ref[3, :, hi] += down_c[...]

    finish(me, acc_ref, own_ref, gather_ref, *extra)

    first, second = pl.ds(0, cut), pl.ds(cut, out_width - cut)

    def block(dev, cols):
        return gather_ref.at[dev, :, cols]

    def move(dev, cols, peer):
        return copy(block(dev, cols), block(dev, cols), peer)

    up_first, down_second = move(me, first, up), move(me, second, down)
    up_second, down_first = move(me, second, up), move(me, first, down)
    to_mate = move(me, pl.ds(0, out_width), mate)
    for c in (up_first, down_second, up_second, down_first, to_mate):
        c.start()
    sends = [to_mate]
    up_first.wait_recv()
    relay_up = move(down, first, up)
    relay_up.start()
    pass_0 = move(down, first, mate)
    pass_0.start()
    down_second.wait_recv()
    relay_down = move(up, second, down)
    relay_down.start()
    pass_1 = move(up, second, mate)
    pass_1.start()
    up_second.wait_recv()
    pass_2 = move(down, second, mate)
    pass_2.start()
    down_first.wait_recv()
    pass_3 = move(up, first, mate)
    pass_3.start()
    far = 2 * far_chip + core
    relay_up.wait_recv()
    pass_4 = move(far, first, mate)
    pass_4.start()
    relay_down.wait_recv()
    pass_5 = move(far, second, mate)
    pass_5.start()
    passes = [pass_0, pass_1, pass_2, pass_3, pass_4, pass_5]
    to_mate.wait_recv()
    for c in passes:
        c.wait_recv()
    all_ref[...] = gather_ref[...].reshape(all_ref.shape).astype(all_ref.dtype)
    for c in (pair + [far_up, far_down, near_up, near_down, sum_up, sum_down, up_first, down_second, up_second,
                      down_first, relay_up, relay_down] + sends + passes):
        c.wait_send()


def all_reduce(finish, collective_id, tp_size, part, extra, extra_specs, out_width, name):
    blocks, rows, width = part.shape
    split = (width // LANES + 1) // 2 * LANES
    chips = tp_size // 2
    f32 = jnp.float32
    return pl.pallas_call(
        functools.partial(reduce_kernel, finish, chips, split, len(extra)),
        out_shape=(jax.ShapeDtypeStruct((blocks * rows, out_width), jnp.bfloat16),
                   jax.ShapeDtypeStruct((rows, out_width), f32)),
        in_specs=[VMEM] + extra_specs,
        out_specs=(VMEM, VMEM),
        scratch_shapes=[
            pltpu.VMEM((chips, rows, width), f32),
            pltpu.VMEM((chips, rows, width), f32),
            pltpu.VMEM((rows, split), f32), pltpu.VMEM((rows, width - split), f32), pltpu.VMEM((rows, split), f32),
            pltpu.VMEM((rows, width - split), f32), pltpu.VMEM((rows, split), f32), pltpu.VMEM((rows, width - split), f32),
            pltpu.VMEM((blocks, rows, out_width), f32),
            pltpu.SemaphoreType.DMA((32,)), pltpu.SemaphoreType.DMA((32,)),
        ],
        compiler_params=pltpu.CompilerParams(collective_id=collective_id, has_side_effects=True,
                                             vmem_limit_bytes=16 << 20),
        cost_estimate=pl.CostEstimate(flops=10 ** 9, transcendentals=0, bytes_accessed=10 ** 7),
        name=name,
    )(part, *extra)


def finish_first(full_width, me, acc_ref, own_ref, gather_ref, h1_ref, norm_ref, alpha_ref, beta_ref):
    width = own_ref.shape[1]
    inv = lax.rsqrt(acc_ref[3, :, pl.ds(width, 1)] / full_width + EPS)
    lin = acc_ref[3, :, pl.ds(0, width)] * inv
    mid = (alpha_ref[0] * h1_ref[me] + beta_ref[0] * lin).astype(jnp.bfloat16).astype(jnp.float32)
    h2 = mid * lax.rsqrt(jnp.mean(mid * mid, axis=-1, keepdims=True) + EPS) * norm_ref[...]
    h2 = h2.astype(jnp.bfloat16).astype(jnp.float32)
    own_ref[...] = h2
    gather_ref[me] = h2


def finish_second(me, acc_ref, own_ref, gather_ref, h2_ref, alpha_ref, beta_ref):
    out = (alpha_ref[1] * h2_ref[...] + beta_ref[1] * acc_ref[3]).astype(jnp.bfloat16).astype(jnp.float32)
    own_ref[...] = out
    gather_ref[me] = out


def attention_kernel(len_ref, h2_ref, watt_ref, cos_ref, sina_ref, sinb_ref, k_ref, v_ref, wout_ref,
                     k_out_ref, v_out_ref, part_ref, q_ref, kn_ref, vn_ref, att_ref):
    step = pl.program_id(0)
    steps = pl.num_programs(0)
    per = k_ref.shape[0]
    batch, width = h2_ref.shape
    group = watt_ref.shape[0] - 2
    dim = watt_ref.shape[2]
    tmax = k_ref.shape[2]

    @pl.when(step == 0)
    def _():
        h2 = h2_ref[...]

        def turn(x):
            return x * cos_ref[...] + pltpu.roll(x, dim - dim // 4, 1) * sina_ref[...] + pltpu.roll(x, dim // 4, 1) * sinb_ref[...]

        q_ref[...] = jnp.zeros_like(q_ref)
        for j in range(group):
            x = jnp.dot(h2, watt_ref[j], preferred_element_type=jnp.float32)
            q_ref[:, j, :] = turn(x)
        kn_ref[...] = turn(jnp.dot(h2, watt_ref[group], preferred_element_type=jnp.float32))
        vn_ref[...] = jnp.dot(h2, watt_ref[group + 1], preferred_element_type=jnp.float32)

    sub = 16
    rows16 = lax.broadcasted_iota(jnp.int32, (sub, dim), 0)
    cols = lax.broadcasted_iota(jnp.int32, (ROWS, tmax), 1)
    scale = dim ** -0.5
    base = step * per
    for ref, out, new in ((k_ref, k_out_ref, kn_ref), (v_ref, v_out_ref, vn_ref)):
        out[...] = ref[...]
        for r in range(per):
            pos = len_ref[base + r]
            start = pl.multiple_of((pos // sub) * sub, sub)
            old = out[r, 0, pl.ds(start, sub), :].astype(jnp.float32)
            row = new[pl.ds(base + r, 1), :]
            out[r, 0, pl.ds(start, sub), :] = jnp.where(rows16 == pos - start, row, old).astype(jnp.bfloat16)
    for r in range(per):
        pos = len_ref[base + r]
        q = q_ref[base + r].astype(jnp.bfloat16)
        s = lax.dot_general(q, k_out_ref[r, 0], (((1,), (1,)), ((), ())), preferred_element_type=jnp.float32) * scale
        s = jnp.where(cols <= pos, s, -jnp.inf)
        e = jnp.exp(s - jnp.max(s, axis=1, keepdims=True))
        p = (e / jnp.sum(e, axis=1, keepdims=True)).astype(jnp.bfloat16)
        att_ref[base + r] = jnp.dot(p, v_out_ref[r, 0], preferred_element_type=jnp.float32)

    @pl.when(step == steps - 1)
    def _():
        rows = jnp.concatenate([att_ref[:, j, :] for j in range(group)], axis=1).astype(jnp.bfloat16)
        tile = 1024
        for c in range(width // tile):
            cs = pl.ds(c * tile, tile)
            piece = jnp.dot(rows, wout_ref[:, cs], preferred_element_type=jnp.float32)
            part_ref[:, :, cs] = piece.reshape(batch // ROWS, ROWS, tile)


def attention(cache_len, h2, w_attn, tables, k_cache, v_cache, w_out):
    batch, width = h2.shape
    _, _, tmax, dim = k_cache.shape
    slots = w_attn.shape[0]
    per = 8
    blocks = batch // ROWS
    cache_spec = pl.BlockSpec((per, 1, tmax, dim), lambda i: (i, 0, 0, 0))

    def whole(x):
        return pl.BlockSpec(x.shape, lambda i: (0,) * x.ndim)

    return pl.pallas_call(
        attention_kernel,
        grid=(batch // per,),
        out_shape=(jax.ShapeDtypeStruct(k_cache.shape, k_cache.dtype),
                   jax.ShapeDtypeStruct(v_cache.shape, v_cache.dtype),
                   jax.ShapeDtypeStruct((blocks, ROWS, width), jnp.float32)),
        in_specs=[SMEM, whole(h2), whole(w_attn)] + [whole(t) for t in tables] + [cache_spec, cache_spec, whole(w_out)],
        out_specs=(cache_spec, cache_spec, pl.BlockSpec((blocks, ROWS, width), lambda i: (0, 0, 0))),
        scratch_shapes=[
            pltpu.VMEM((batch, ROWS, dim), jnp.float32),
            pltpu.VMEM((batch, dim), jnp.float32),
            pltpu.VMEM((batch, dim), jnp.float32),
            pltpu.VMEM((batch, ROWS, dim), jnp.float32),
        ],
        compiler_params=pltpu.CompilerParams(vmem_limit_bytes=60 << 20),
        cost_estimate=pl.CostEstimate(flops=2 * batch * width * dim * slots * 2, transcendentals=0,
                                      bytes_accessed=4 * k_cache.size * 2),
        name="attention",
    )(cache_len, h2, w_attn, *tables, k_cache, v_cache, w_out)


def rotary_tables(cache_len, dim):
    rot = dim // 2
    half = rot // 2
    inv_freq = ROPE_BASE ** (-2.0 * jnp.arange(half, dtype=jnp.float32) / rot)
    angles = cache_len.astype(jnp.float32)[:, None] * inv_freq[None, :]
    cosine, sine = jnp.cos(angles), jnp.sin(angles)
    ones = jnp.ones((cache_len.shape[0], dim - rot), jnp.float32)
    zero = jnp.zeros_like(sine)
    return (jnp.concatenate([cosine, cosine, ones], axis=1),
            jnp.concatenate([-sine, zero, 0 * ones], axis=1),
            jnp.concatenate([zero, sine, 0 * ones], axis=1))


def solution(mesh):
    tp_size = mesh.shape['tp']
    row_spec = P('dp', None)
    cache_spec = P('dp', 'tp', None, None)
    in_specs = (row_spec, P('dp'), cache_spec, cache_spec, cache_spec, P(None), P(None, None, 'tp', None),
                P(None, 'tp', None), P('tp'), P('tp', None), P('tp', None, None), P(None),
                P(None, 'tp', None, None), P('tp', None, None), P(None), P(None))
    out_specs = (row_spec, cache_spec, cache_spec, cache_spec)

    def local_step(hidden, cache_len, lin_state, k_cache, v_cache, norm_first, w_qkv, w_gate, slopes, out_norm,
                   w_out_lin, norm_second, w_attn, w_out_attn, mix_alpha, mix_beta):
        width = hidden.shape[1]
        dim = k_cache.shape[3]
        full_width = w_out_lin.shape[0] * dim * tp_size
        tables = rotary_tables(cache_len, dim)
        state_out, part, h1 = lightning(hidden, norm_first, w_qkv, w_gate, lin_state, slopes, out_norm, w_out_lin)
        h2, h2_own = all_reduce(functools.partial(finish_first, full_width), 0, tp_size, part,
                                (h1, norm_second.reshape(1, width), mix_alpha, mix_beta), [VMEM, VMEM, SMEM, SMEM],
                                width, "reduce_first")
        w_heads = w_attn.transpose(1, 2, 0, 3).reshape(w_attn.shape[2], width, dim)
        k_out, v_out, part = attention(cache_len, h2, w_heads, tables, k_cache, v_cache,
                                       w_out_attn.reshape(w_out_attn.shape[0] * dim, width))
        hidden_out, _ = all_reduce(finish_second, 1, tp_size, part, (h2_own, mix_alpha, mix_beta), [VMEM, SMEM, SMEM],
                                   width, "reduce_second")
        return hidden_out, state_out, k_out, v_out

    return jax.shard_map(local_step, mesh=mesh, in_specs=in_specs, out_specs=out_specs, check_vma=False)
```

time: 216 us -> 123 us (0.57)
  Pallas kernels: 0 us -> 113 us
  waiting for transfers between devices: 108 us -> 0 us
  matrix products: 45.9 us -> 0 us
  other arithmetic: 28.9 us -> 1.58 us
  blocking collectives: 13.6 us -> 0 us
  between operations: 14.3 us -> 0.72 us
  local copies, waits for them, and re-layouts: 2.73 us -> 7.06 us
    pallas_call x0 -> x4, Pallas kernels: none -> 113 us  [the longest x2 46.5 us: all_reduce(): pl.pallas_call(functools.partial(reduce_kernel, finish, chips, split, len...]
    psum x2 -> x0, waiting for transfers between devices: 108 us -> none  [the longest x1 54.5 us: local_step(): attn_out = lax.psum(attn_part, 'tp')]
    dot_general x7 -> x0, matrix products: 45.9 us -> none  [the longest x1 10.4 us: local_step(): jnp.einsum('bd,dchk->bchk', h_first, w_qkv, preferred_element_type=jnp.fl...]
    psum x1 -> x0, blocking collectives: 13.6 us -> none  [local_step(): sq_sum = lax.psum(jnp.sum(lin_attn * lin_attn, axis=(1, 2)), 'tp')]
    select_n x1 -> x0, other arithmetic: 9.47 us -> none  [local_step(): k_out = jnp.where(write_mask, key_new, k_cache)]
    add x1 -> x0, other arithmetic: 9.46 us -> none  [local_step(): decay_rate * lin_state]
    reduce_sum x3 -> x0, other arithmetic: 4.56 us -> none  [the longest x2 4.45 us: rms_scale(): jnp.mean(wide_vals * wide_vals, axis=-1, keepdims=True) + EPS]
    unnamed x18 -> x15, local copies, waits for them, and re-layouts: 1.17 us -> 5.63 us
  transfers between devices with their start and end apart: 2 -> 0, of which waited for: 2 -> 0; matrix products, arithmetic and copies ran while one was open for 1% -> 0% of each run, Pallas kernels for 0% -> 0%
where the time goes in v1:
time: 123 us; the launch traced here: 122 us
  Pallas kernels  113 us (92%)
  local copies, waits for them, and re-layouts  7.06 us (6%)
  other arithmetic  1.58 us (1%)
    pallas_call x2, Pallas kernels, all_reduce(): pl.pallas_call(functools.partial(reduce_kernel, finish, chips, split, len...  46.5 us
    pallas_call x1, Pallas kernels, attention(): pl.pallas_call(attention_kernel, grid=(batch // per,), out_shape=(jax.Sha...  33.5 us
    pallas_call x1, Pallas kernels, lightning(): pl.pallas_call(lightning_kernel, grid=(heads,), out_shape=(jax.ShapeDtype...  33 us
    unnamed x15, local copies, waits for them, and re-layouts  5.63 us

profile of v1, /device:TPU:113, one launch (start us, length us, event | category | flops | bytes accessed | tf_op | source)
XLA Modules:
  0.0 122.4 jit_solution(2211047545563511119)
XLA Ops:
  0.6 0.7 convert_element_type.3
  1.3 0.1 pad.8.clone
  1.4 0.1 pad.5.clone
  1.5 1.3 %reshape.30.onorm_ref = f32[5,1,128]{2,1,0:T(1,128)} reshape(f32[5,128]{1,0:T(8,128)} %param.25) | data formatting | bytes 5120 | tf_op jit(solution)/shard_map/reshape | solution.py:127
  2.7 0.2 multiply_sine_fusion
  2.9 0.7 maximum_maximum_fusion.2
  3.7 0.0 copy-start.4
  3.7 0.0 copy-start.5
  3.7 0.0 copy-start.6
  3.7 33.0 %lightning.1 = (f32[64,5,128,128]{3,2,1,0:T(8,128)}, f32[8,8,5248]{2,1,0:T(8,128)}, f32[8,8,5120]{2,1,0:T(8,128)}) custom-call(f32[5]{0:T(128)} %slopes_ref.1, bf16[64,5120]{1,0:T(8,128)(2,1)} %hidden_ref.1, f32[1,5120]{1,0:T(1,128)} %bitcast.13, bf16[3,5,5120,128]{3,2,1,0:T(8,128)(2,1)} %bitcast.9, bf16[5,5120,128]{2,1,0:T(8,128)(2,1)} %bitcast.11, ...), custom_call_target="tpu_custom_call" | custom-call | flops 2097152000 | bytes 74711040 | tf_op jit(solution)/shard_map/lightning/pallas_call | solution.py:93
  36.7 0.0 copy-done.4
  36.7 0.0 copy-done.5
  36.7 0.0 copy-done.6
  36.7 0.0 copy-start.1
  36.7 1.3 %copy-done.1 = f32[8,8,5248]{2,1,0:T(8,128)S(1)} copy-done((f32[8,8,5248]{2,1,0:T(8,128)S(1)}, f32[8,8,5248]{2,1,0:T(8,128)}, u32[]{:S(2)}) %copy-start.1) | copy-done | bytes 1343512
  38.0 1.3 %copy-done.3 = f32[8,8,5120]{2,1,0:T(8,128)S(1)} copy-done((f32[8,8,5120]{2,1,0:T(8,128)S(1)}, f32[8,8,5120]{2,1,0:T(8,128)}, u32[]{:S(2)}) %copy-start.3) | copy-done | bytes 1310744
  39.4 24.8 %reduce_first.1 = (bf16[64,5120]{1,0:T(8,128)(2,1)S(1)}, f32[8,5120]{1,0:T(8,128)S(1)}) custom-call(f32[8,8,5248]{2,1,0:T(8,128)S(1)} %copy-done.1, f32[8,8,5120]{2,1,0:T(8,128)S(1)} %copy-done.3, f32[1,5120]{1,0:T(1,128)S(1)} %bitcast.8, f32[2]{0:T(128)S(1)} %copy-done.5, f32[2]{0:T(128)S(1)} %copy-done.6), custom_call_target="tpu_custom_call" | custom-call | flops 1000000000 | bytes 10000000 | tf_op jit(solution)/shard_map/reduce_first/pallas_call | solution.py:247
  64.1 0.0 copy-start
  64.2 0.8 copy-done
  65.0 33.5 %attention.1 = (bf16[64,1,512,128]{3,2,1,0:T(8,128)(2,1)}, bf16[64,1,512,128]{3,2,1,0:T(8,128)(2,1)}, f32[8,8,5120]{2,1,0:T(8,128)}) custom-call(s32[64]{0:T(128)} %len_ref.1, bf16[64,5120]{1,0:T(8,128)(2,1)} %copy-done, bf16[7,5120,128]{2,1,0:T(8,128)(2,1)} %bitcast.10, f32[64,128]{1,0:T(8,128)} %get-tuple-element.27.cos_ref, ...), custom_call_target="tpu_custom_call" | custom-call | flops 1174405120 | bytes 33554432 | tf_op jit(solution)/shard_map/attention/pallas_call | solution.py:352
  98.5 0.0 copy-start.2
  98.5 1.3 %copy-done.2 = f32[8,8,5120]{2,1,0:T(8,128)S(1)} copy-done((f32[8,8,5120]{2,1,0:T(8,128)S(1)}, f32[8,8,5120]{2,1,0:T(8,128)}, u32[]{:S(2)}) %copy-start.2) | copy-done | bytes 1310744
  99.8 21.7 %reduce_second.1 = (bf16[64,5120]{1,0:T(8,128)(2,1)S(1)}, f32[8,5120]{1,0:T(8,128)}) custom-call(f32[8,8,5120]{2,1,0:T(8,128)S(1)} %copy-done.2, f32[8,5120]{1,0:T(8,128)S(1)} %get-tuple-element.17.refs_0_, f32[2]{0:T(128)S(1)} %copy-done.5, f32[2]{0:T(128)S(1)} %copy-done.6), custom_call_target="tpu_custom_call" | custom-call | flops 1000000000 | bytes 10000000 | tf_op jit(solution)/shard_map/reduce_second/pallas_call | solution.py:247
  121.6 0.8 copy.21
  (5 shorter events, 0.0 us)
Async XLA Ops:
  3.7 33.0 %copy-start.4 = (f32[5120]{0:T(1024)S(1)}, f32[5120]{0:T(1024)}, u32[]{:S(2)}) copy-start(f32[5120]{0:T(1024)} %param.27) | copy-start | bytes 61444
  3.7 33.0 %copy-start.5 = (f32[2]{0:T(128)S(1)}, f32[2]{0:T(128)}, u32[]{:S(2)}) copy-start(f32[2]{0:T(128)} %refs_1_.1) | copy-start | bytes 28
  3.7 33.0 %copy-start.6 = (f32[2]{0:T(128)S(1)}, f32[2]{0:T(128)}, u32[]{:S(2)}) copy-start(f32[2]{0:T(128)} %refs_2_.3) | copy-start | bytes 28
  36.7 1.3 %copy-start.1 = (f32[8,8,5248]{2,1,0:T(8,128)S(1)}, f32[8,8,5248]{2,1,0:T(8,128)}, u32[]{:S(2)}) copy-start(f32[8,8,5248]{2,1,0:T(8,128)} %get-tuple-element.13.part_ref) | copy-start | bytes 4030468
  38.0 1.3 %copy-start.3 = (f32[8,8,5120]{2,1,0:T(8,128)S(1)}, f32[8,8,5120]{2,1,0:T(8,128)}, u32[]{:S(2)}) copy-start(f32[8,8,5120]{2,1,0:T(8,128)} %get-tuple-element.14.refs_0_) | copy-start | bytes 3932164
  64.1 0.8 copy-start
  98.5 1.3 %copy-start.2 = (f32[8,8,5120]{2,1,0:T(8,128)S(1)}, f32[8,8,5120]{2,1,0:T(8,128)}, u32[]{:S(2)}) copy-start(f32[8,8,5120]{2,1,0:T(8,128)} %get-tuple-element.16.part_ref) | copy-start | bytes 3932164

commit v2 on v1

v2 whole, which is shorter than its diff:
```python
import functools

import jax
import jax.numpy as jnp
import numpy as np
from jax import lax
from jax.experimental import pallas as pl
from jax.experimental.pallas import tpu as pltpu
from jax.sharding import PartitionSpec as P

EPS = 1e-5
ROPE_BASE = 10000000.0
MESH = pl.DeviceIdType.MESH
VMEM = pl.BlockSpec(memory_space=pltpu.VMEM)
SMEM = pl.BlockSpec(memory_space=pltpu.SMEM)
HBM = pl.BlockSpec(memory_space=pltpu.HBM)
ROWS = 8
LANES = 128


CHUNKS = 4
WINDOW = 9
SLOTS = 3


def lightning_kernel(slopes_hbm, len_hbm, freq_hbm, norm_hbm, onorm_hbm, hidden_hbm, wqkv_hbm, wgate_hbm, state_hbm, wout_hbm,
                     state_out_hbm, part_ref, h1_out_ref, table_ref, pos_ref,
                     slopes_ref, len_ref, freq_ref, norm_ref, onorm_ref, hidden_ref, wqkv_ref, wgate_ref, state_ref, wout_ref, h1_ref, sq_ref, kt_ref, qt_ref, v_ref, o_ref,
                     small_sem, w_sem, in_sem, out_sem):
    batch, width = hidden_ref.shape
    heads, dim = onorm_ref.shape
    rows = batch // CHUNKS

    def state_in(h, c):
        return pltpu.make_async_copy(state_hbm.at[pl.ds(c * rows, rows), h], state_ref.at[h % SLOTS, pl.ds(c * rows, rows)], in_sem.at[h % SLOTS, c])

    def state_out(h, c):
        return pltpu.make_async_copy(state_ref.at[h % SLOTS, pl.ds(c * rows, rows)], state_out_hbm.at[pl.ds(c * rows, rows), h],
                                     out_sem.at[h % SLOTS, c])

    small = [pltpu.make_async_copy(src, dst, small_sem.at[i])
             for i, (src, dst) in enumerate(((len_hbm, len_ref), (freq_hbm, freq_ref), (hidden_hbm, hidden_ref), (norm_hbm, norm_ref),
                                             (slopes_hbm, slopes_ref), (onorm_hbm, onorm_ref)))]
    def piece(h, j):
        if j < 3:
            return pltpu.make_async_copy(wqkv_hbm.at[j, h], wqkv_ref.at[h % 2, j], w_sem.at[h % 2, j])
        if j == 3:
            return pltpu.make_async_copy(wgate_hbm.at[h], wgate_ref.at[h % 2], w_sem.at[h % 2, 3])
        if j < 4 + CHUNKS:
            return state_in(h, j - 4)
        return pltpu.make_async_copy(wout_hbm.at[h], wout_ref.at[h % 2], w_sem.at[h % 2, 4])

    pieces = 5 + CHUNKS

    def take(h, j):
        piece(h, j).wait()
        ahead, later = (j + WINDOW) // pieces, (j + WINDOW) % pieces

        if 4 <= later < 4 + CHUNKS:
            @pl.when((h + ahead >= SLOTS) & (h + ahead < heads))
            def _():
                state_out(h + ahead - SLOTS, later - 4).wait()

        @pl.when(h + ahead < heads)
        def _():
            piece(h + ahead, later).start()

    for c in small:
        c.start()
    for i in range(WINDOW):
        piece(i // pieces, i % pieces).start()

    for c in small[:2]:
        c.wait()
    for r in range(batch):
        pos_ref[r] = jnp.full((ROWS, LANES), len_ref[r], jnp.int32)
    angle = pos_ref[:, 0, :].astype(jnp.float32) * freq_ref[...]
    cosine, sine = jnp.cos(angle), jnp.sin(angle)
    lane = lax.broadcasted_iota(jnp.int32, angle.shape, 1)
    table_ref[0] = jnp.where(lane < dim // 2, cosine, 1.0)
    table_ref[1] = jnp.where(lane < dim // 4, -sine, 0.0)
    table_ref[2] = jnp.where((lane >= dim // 4) & (lane < dim // 2), sine, 0.0)

    for c in small[2:]:
        c.wait()
    x = hidden_ref[...].astype(jnp.float32)
    h1 = x * lax.rsqrt(jnp.mean(x * x, axis=-1, keepdims=True) + EPS) * norm_ref[...]
    h1 = h1.astype(jnp.bfloat16)
    h1_ref[...] = h1
    h1_out_ref[...] = h1.astype(jnp.float32).reshape(h1_out_ref.shape)
    sq_ref[...] = jnp.zeros_like(sq_ref)
    part_ref[...] = jnp.zeros_like(part_ref)

    def silu(x):
        return (x * jax.nn.sigmoid(x)).astype(jnp.bfloat16).astype(jnp.float32)

    def one_head(head, _):
        def project(w):
            return jnp.dot(h1_ref[...], w, preferred_element_type=jnp.float32)

        take(head, 0)
        q = silu(project(wqkv_ref[head % 2, 0]))
        take(head, 1)
        k = silu(project(wqkv_ref[head % 2, 1]))
        take(head, 2)
        v = silu(project(wqkv_ref[head % 2, 2]))
        take(head, 3)
        gate = jax.nn.sigmoid(project(wgate_ref[head % 2]))
        v_ref[...] = v
        kt = k.T
        qt = q.T
        for i in range(batch // ROWS):
            kt_ref[i] = kt[:, i * ROWS:(i + 1) * ROWS]
            qt_ref[i] = qt[:, i * ROWS:(i + 1) * ROWS]
        decay = jnp.exp(-jnp.full((1, LANES), slopes_ref[head], jnp.float32))

        def block(i, _):
            kb, qb = kt_ref[i], qt_ref[i]
            base = pl.multiple_of(i * ROWS, ROWS)
            vb = v_ref[pl.ds(base, ROWS), :]
            outs = []
            for r in range(ROWS):
                new = decay * state_ref[head % SLOTS, base + r] + kb[:, r:r + 1] * vb[r:r + 1, :]
                state_ref[head % SLOTS, base + r] = new
                outs.append(jnp.sum(qb[:, r:r + 1] * new, axis=0, keepdims=True))
            o_ref[pl.ds(base, ROWS), :] = jnp.concatenate(outs, axis=0)
            return 0

        per = rows // ROWS

        for c in range(CHUNKS):
            take(head, 4 + c)
            lax.fori_loop(c * per, (c + 1) * per, block, 0)
            state_out(head, c).start()
        o = o_ref[...]
        sq_ref[...] += jnp.broadcast_to(jnp.sum(o * o, axis=1, keepdims=True), sq_ref.shape)
        gated = (o * onorm_ref[pl.ds(head, 1), :] * gate).astype(jnp.bfloat16)
        take(head, pieces - 1)
        tile = 1024
        for c in range(width // tile):
            cols = pl.ds(c * tile, tile)
            piece = jnp.dot(gated, wout_ref[head % 2, :, cols], preferred_element_type=jnp.float32)
            part_ref[:, :, cols] += piece.reshape(batch // ROWS, ROWS, tile)
        return 0

    lax.fori_loop(0, heads, one_head, 0)
    part_ref[:, :, pl.ds(width, LANES)] = sq_ref[...].reshape(batch // ROWS, ROWS, LANES)
    for h in range(max(heads - SLOTS, 0), heads):
        for c in range(CHUNKS):
            state_out(h, c).wait()


def in_hbm(x):
    return pltpu.with_memory_space_constraint(x, pltpu.HBM)


def in_vmem(x):
    return pltpu.with_memory_space_constraint(x, pltpu.VMEM)


def lightning(hidden, cache_len, freq, norm_first, w_qkv, w_gate, lin_state, slopes, out_norm, w_out_lin):
    batch, width = hidden.shape
    heads, dim = out_norm.shape
    blocks = batch // ROWS
    f32, bf16 = jnp.float32, jnp.bfloat16
    return pl.pallas_call(
        lightning_kernel,
        out_shape=(pltpu.HBM(lin_state.shape, f32),
                   pltpu.VMEM((blocks, ROWS, width + LANES), f32),
                   pltpu.VMEM((blocks, ROWS, width), f32),
                   pltpu.VMEM((3, batch, dim), f32),
                   pltpu.VMEM((batch, ROWS, LANES), jnp.int32)),
        in_specs=[HBM] * 10,
        out_specs=(HBM, VMEM, VMEM, VMEM, VMEM),
        scratch_shapes=[
            pltpu.SMEM((heads,), f32),
            pltpu.SMEM((batch,), jnp.int32),
            pltpu.VMEM((1, dim), f32),
            pltpu.VMEM((1, width), f32),
            pltpu.VMEM((heads, dim), f32),
            pltpu.VMEM((batch, width), bf16),
            pltpu.VMEM((2, 3, width, dim), bf16),
            pltpu.VMEM((2, width, dim), bf16),
            pltpu.VMEM((SLOTS, batch, dim, dim), f32),
            pltpu.VMEM((2, dim, width), bf16),
            pltpu.VMEM((batch, width), bf16),
            pltpu.VMEM((batch, LANES), f32),
            pltpu.VMEM((blocks, dim, ROWS), f32),
            pltpu.VMEM((blocks, dim, ROWS), f32),
            pltpu.VMEM((batch, dim), f32),
            pltpu.VMEM((batch, dim), f32),
            pltpu.SemaphoreType.DMA((6,)),
            pltpu.SemaphoreType.DMA((2, 5)),
            pltpu.SemaphoreType.DMA((SLOTS, CHUNKS)),
            pltpu.SemaphoreType.DMA((SLOTS, CHUNKS)),
        ],
        compiler_params=pltpu.CompilerParams(vmem_limit_bytes=36 << 20),
        cost_estimate=pl.CostEstimate(flops=2 * batch * width * heads * dim * 5, transcendentals=0,
                                      bytes_accessed=2 * lin_state.size * 4 + 10 * heads * dim * width),
        name="lightning",
    )(in_hbm(slopes), in_hbm(cache_len), in_hbm(freq), in_hbm(norm_first.reshape(1, width)), in_hbm(out_norm), in_hbm(hidden), in_hbm(w_qkv.transpose(1, 2, 0, 3)),
      in_hbm(w_gate.transpose(1, 0, 2)), in_hbm(lin_state), in_hbm(w_out_lin))


def reduce_kernel(finish, chips, split, n_extra, part_ref, *refs):
    extra, (all_ref, own_ref), scratch = refs[:n_extra], refs[n_extra:n_extra + 2], refs[n_extra + 2:]
    pair_ref, acc_ref, up_a, up_b, up_c, down_a, down_b, down_c, gather_ref, send_sem, recv_sem = scratch
    width = part_ref.shape[2]
    out_width = gather_ref.shape[2]
    cut = out_width // 2
    me = lax.axis_index("tp")
    chip, core = me // 2, me % 2
    mate = 2 * chip + (1 - core)
    next_chip, prev_chip, far_chip = (chip + 1) % chips, (chip + chips - 1) % chips, (chip + 2) % chips
    up, down = 2 * next_chip + core, 2 * prev_chip + core

    barrier = pltpu.get_barrier_semaphore()
    for peer in (mate, up, down):
        pl.semaphore_signal(barrier, inc=1, device_id={"tp": peer}, device_id_type=MESH)
    pl.semaphore_wait(barrier, 3)

    counter = iter(range(64))

    def copy(src, dst, peer):
        i = next(counter)
        return pltpu.make_async_remote_copy(src_ref=src, dst_ref=dst, send_sem=send_sem.at[i], recv_sem=recv_sem.at[i],
                                            device_id={"tp": peer}, device_id_type=MESH)

    lo, hi = pl.ds(0, split), pl.ds(split, width - split)

    pair = [copy(part_ref.at[2 * t + (1 - core)], pair_ref.at[s], mate)
            for s, t in enumerate((far_chip, next_chip, prev_chip, chip))]
    for c in pair:
        c.start()
    pair[0].wait_recv()
    acc_ref[0] = part_ref[2 * far_chip + core] + pair_ref[0]
    far_up = copy(acc_ref.at[0, :, lo], up_a, up)
    far_down = copy(acc_ref.at[0, :, hi], down_a, down)
    far_up.start()
    far_down.start()
    pair[1].wait_recv()
    acc_ref[1] = part_ref[2 * next_chip + core] + pair_ref[1]
    near_up = copy(acc_ref.at[1, :, hi], up_b, up)
    near_up.start()
    pair[2].wait_recv()
    acc_ref[2] = part_ref[2 * prev_chip + core] + pair_ref[2]
    near_down = copy(acc_ref.at[2, :, lo], down_b, down)
    near_down.start()
    far_up.wait_recv()
    acc_ref[1, :, lo] += up_a[...]
    sum_up = copy(acc_ref.at[1, :, lo], up_c, up)
    sum_up.start()
    far_down.wait_recv()
    acc_ref[2, :, hi] += down_a[...]
    sum_down = copy(acc_ref.at[2, :, hi], down_c, down)
    sum_down.start()
    pair[3].wait_recv()
    acc_ref[3] = part_ref[me] + pair_ref[3]
    near_up.wait_recv()
    acc_ref[3, :, hi] += up_b[...]
    near_down.wait_recv()
    acc_ref[3, :, lo] += down_b[...]
    sum_up.wait_recv()
    acc_ref[3, :, lo] += up_c[...]
    sum_down.wait_recv()
    acc_ref[3, :, hi] += down_c[...]

    finish(me, acc_ref, own_ref, gather_ref, *extra)

    first, second = pl.ds(0, cut), pl.ds(cut, out_width - cut)

    def block(dev, cols):
        return gather_ref.at[dev, :, cols]

    def move(dev, cols, peer):
        return copy(block(dev, cols), block(dev, cols), peer)

    up_first, down_second = move(me, first, up), move(me, second, down)
    up_second, down_first = move(me, second, up), move(me, first, down)
    to_mate = move(me, pl.ds(0, out_width), mate)
    for c in (up_first, down_second, up_second, down_first, to_mate):
        c.start()
    sends = [to_mate]
    up_first.wait_recv()
    relay_up = move(down, first, up)
    relay_up.start()
    pass_0 = move(down, first, mate)
    pass_0.start()
    down_second.wait_recv()
    relay_down = move(up, second, down)
    relay_down.start()
    pass_1 = move(up, second, mate)
    pass_1.start()
    up_second.wait_recv()
    pass_2 = move(down, second, mate)
    pass_2.start()
    down_first.wait_recv()
    pass_3 = move(up, first, mate)
    pass_3.start()
    far = 2 * far_chip + core
    relay_up.wait_recv()
    pass_4 = move(far, first, mate)
    pass_4.start()
    relay_down.wait_recv()
    pass_5 = move(far, second, mate)
    pass_5.start()
    passes = [pass_0, pass_1, pass_2, pass_3, pass_4, pass_5]
    to_mate.wait_recv()
    for c in passes:
        c.wait_recv()
    all_ref[...] = gather_ref[...].reshape(all_ref.shape).astype(all_ref.dtype)
    for c in (pair + [far_up, far_down, near_up, near_down, sum_up, sum_down, up_first, down_second, up_second,
                      down_first, relay_up, relay_down] + sends + passes):
        c.wait_send()


def all_reduce(finish, collective_id, tp_size, part, extra, extra_specs, out_width, name):
    blocks, rows, width = part.shape
    split = (width // LANES + 1) // 2 * LANES
    chips = tp_size // 2
    f32 = jnp.float32
    return pl.pallas_call(
        functools.partial(reduce_kernel, finish, chips, split, len(extra)),
        out_shape=(jax.ShapeDtypeStruct((blocks * rows, out_width), jnp.bfloat16),
                   jax.ShapeDtypeStruct((rows, out_width), f32)),
        in_specs=[VMEM] + extra_specs,
        out_specs=(VMEM, VMEM),
        scratch_shapes=[
            pltpu.VMEM((chips, rows, width), f32),
            pltpu.VMEM((chips, rows, width), f32),
            pltpu.VMEM((rows, split), f32), pltpu.VMEM((rows, width - split), f32), pltpu.VMEM((rows, split), f32),
            pltpu.VMEM((rows, width - split), f32), pltpu.VMEM((rows, split), f32), pltpu.VMEM((rows, width - split), f32),
            pltpu.VMEM((blocks, rows, out_width), f32),
            pltpu.SemaphoreType.DMA((32,)), pltpu.SemaphoreType.DMA((32,)),
        ],
        compiler_params=pltpu.CompilerParams(collective_id=collective_id, has_side_effects=True,
                                             vmem_limit_bytes=8 << 20),
        cost_estimate=pl.CostEstimate(flops=10 ** 11, transcendentals=0, bytes_accessed=10 ** 8),
        name=name,
    )(part, *extra)


def finish_first(full_width, me, acc_ref, own_ref, gather_ref, h1_ref, norm_ref, alpha_ref, beta_ref):
    width = own_ref.shape[1]
    inv = lax.rsqrt(acc_ref[3, :, pl.ds(width, 1)] / full_width + EPS)
    lin = acc_ref[3, :, pl.ds(0, width)] * inv
    mid = (alpha_ref[0] * h1_ref[me] + beta_ref[0] * lin).astype(jnp.bfloat16).astype(jnp.float32)
    h2 = mid * lax.rsqrt(jnp.mean(mid * mid, axis=-1, keepdims=True) + EPS) * norm_ref[...]
    h2 = h2.astype(jnp.bfloat16).astype(jnp.float32)
    own_ref[...] = h2
    gather_ref[me] = h2


def finish_second(me, acc_ref, own_ref, gather_ref, h2_ref, alpha_ref, beta_ref):
    out = (alpha_ref[1] * h2_ref[...] + beta_ref[1] * acc_ref[3]).astype(jnp.bfloat16).astype(jnp.float32)
    own_ref[...] = out
    gather_ref[me] = out


def attention_kernel(len_ref, h2_ref, table_ref, pos_ref, watt_ref, k_ref, v_ref, wout_ref,
                     k_out_hbm, v_out_hbm, part_ref, q_ref, kn_ref, vn_ref, att_ref, patch_ref, bulk_sem, patch_sem):
    batch, width = h2_ref.shape
    group = watt_ref.shape[0] - 2
    dim = watt_ref.shape[2]
    tmax = k_ref.shape[2]
    per = 8
    sub = 16
    blocks = batch // per

    def bulk(i, which):
        src, dst = ((k_ref, k_out_hbm), (v_ref, v_out_hbm))[which]
        rows = pl.ds(i * per, per)
        return pltpu.make_async_copy(src.at[rows], dst.at[rows], bulk_sem.at[i, which])

    def patch(b, which):
        dst = (k_out_hbm, v_out_hbm)[which]
        start = pl.multiple_of((len_ref[b] // sub) * sub, sub)
        return pltpu.make_async_copy(patch_ref.at[which, b], dst.at[b, 0, pl.ds(start, sub)], patch_sem.at[b, which])

    for i in range(blocks):
        for which in range(2):
            bulk(i, which).start()

    h2 = h2_ref[...]

    def turn(x):
        return (x * table_ref[0] + pltpu.roll(x, dim - dim // 4, 1) * table_ref[1] + pltpu.roll(x, dim // 4, 1) * table_ref[2])

    q_ref[...] = jnp.zeros_like(q_ref)
    for j in range(group):
        q_ref[:, j, :] = turn(jnp.dot(h2, watt_ref[j], preferred_element_type=jnp.float32))
    kn_ref[...] = turn(jnp.dot(h2, watt_ref[group], preferred_element_type=jnp.float32)).astype(jnp.bfloat16).astype(jnp.float32)
    vn_ref[...] = jnp.dot(h2, watt_ref[group + 1], preferred_element_type=jnp.float32).astype(jnp.bfloat16).astype(jnp.float32)

    rows16 = lax.broadcasted_iota(jnp.int32, (sub, dim), 0)
    flat = per * ROWS
    cols = lax.broadcasted_iota(jnp.int32, (flat, tmax), 1)
    scale = dim ** -0.5

    def spread(rows):
        return jnp.concatenate([jnp.broadcast_to(rows[r:r + 1, :], (ROWS, dim)) for r in range(per)], axis=0)

    def block(i, _):
        base = pl.multiple_of(i * per, per)
        news = [kn_ref[pl.ds(base, per), :], vn_ref[pl.ds(base, per), :]]
        for r in range(per):
            b = base + r
            pos = len_ref[b]
            start = pl.multiple_of((pos // sub) * sub, sub)
            for which, ref in ((0, k_ref), (1, v_ref)):
                old = ref[b, 0, pl.ds(start, sub), :].astype(jnp.float32)
                patch_ref[which, b] = jnp.where(rows16 == pos - start, news[which][r:r + 1, :], old).astype(jnp.bfloat16)
        q = q_ref[pl.ds(base, per)].reshape(flat, dim)
        q_bf = q.astype(jnp.bfloat16)
        s_new = jnp.sum(q_bf.astype(jnp.float32) * spread(news[0]), axis=1, keepdims=True)
        scores = [lax.dot_general(q_bf[r * ROWS:(r + 1) * ROWS], k_ref[base + r, 0], (((1,), (1,)), ((), ())),
                                  preferred_element_type=jnp.float32) for r in range(per)]
        s = jnp.concatenate(scores, axis=0)
        pos = pos_ref[pl.ds(base, per)].reshape(flat, LANES)
        pos = jnp.concatenate([pos] * (tmax // LANES), axis=1)
        at_pos = cols == pos
        s = jnp.where(at_pos, s_new, s) * scale
        s = jnp.where(cols <= pos, s, -jnp.inf)
        e = jnp.exp(s - jnp.max(s, axis=1, keepdims=True))
        p = (e * (1.0 / jnp.sum(e, axis=1, keepdims=True))).astype(jnp.bfloat16).astype(jnp.float32)
        p_new = jnp.sum(jnp.where(at_pos, p, 0.0), axis=1, keepdims=True)
        p_old = jnp.where(at_pos, 0.0, p).astype(jnp.bfloat16)
        outs = [jnp.dot(p_old[r * ROWS:(r + 1) * ROWS], v_ref[base + r, 0], preferred_element_type=jnp.float32)
                for r in range(per)]
        att = jnp.concatenate(outs, axis=0) + p_new * spread(news[1])
        att_ref[pl.ds(base, per)] = att.reshape(per, ROWS, dim)
        for which in range(2):
            bulk(i, which).wait()
        for r in range(per):
            for which in range(2):
                patch(base + r, which).start()
        return 0

    lax.fori_loop(0, blocks, block, 0)
    rows = jnp.concatenate([att_ref[:, j, :] for j in range(group)], axis=1).astype(jnp.bfloat16)
    tile = 1024
    for c in range(width // tile):
        cs = pl.ds(c * tile, tile)
        piece = jnp.dot(rows, wout_ref[:, cs], preferred_element_type=jnp.float32)
        part_ref[:, :, cs] = piece.reshape(batch // ROWS, ROWS, tile)

    def finish(b, _):
        for which in range(2):
            patch(b, which).wait()
        return 0

    lax.fori_loop(0, batch, finish, 0)


def attention(cache_len, h2, w_attn, tables, positions, k_cache, v_cache, w_out):
    batch, width = h2.shape
    _, _, tmax, dim = k_cache.shape
    slots = w_attn.shape[0]
    blocks = batch // ROWS
    return pl.pallas_call(
        attention_kernel,
        out_shape=(pltpu.HBM(k_cache.shape, k_cache.dtype), pltpu.HBM(v_cache.shape, v_cache.dtype),
                   pltpu.VMEM((blocks, ROWS, width), jnp.float32)),
        in_specs=[SMEM] + [VMEM] * 7,
        out_specs=(HBM, HBM, VMEM),
        scratch_shapes=[
            pltpu.VMEM((batch, ROWS, dim), jnp.float32),
            pltpu.VMEM((batch, dim), jnp.float32),
            pltpu.VMEM((batch, dim), jnp.float32),
            pltpu.VMEM((batch, ROWS, dim), jnp.float32),
            pltpu.VMEM((2, batch, 16, dim), k_cache.dtype),
            pltpu.SemaphoreType.DMA((batch // 8, 2)),
            pltpu.SemaphoreType.DMA((batch, 2)),
        ],
        compiler_params=pltpu.CompilerParams(vmem_limit_bytes=8 << 20),
        cost_estimate=pl.CostEstimate(flops=2 * batch * width * dim * slots * 2, transcendentals=0,
                                      bytes_accessed=4 * k_cache.size * 2),
        name="attention",
    )(cache_len, h2, tables, positions, in_vmem(w_attn), in_vmem(k_cache), in_vmem(v_cache), in_vmem(w_out))


def rotary_freq(dim):
    rot = dim // 2
    half = rot // 2
    freq = ROPE_BASE ** (-2.0 * np.arange(half) / rot)
    return jnp.asarray(np.concatenate([freq, freq, np.zeros(dim - rot)])[None, :], jnp.float32)


def solution(mesh):
    tp_size = mesh.shape['tp']
    row_spec = P('dp', None)
    cache_spec = P('dp', 'tp', None, None)
    in_specs = (row_spec, P('dp'), cache_spec, cache_spec, cache_spec, P(None), P(None, None, 'tp', None),
                P(None, 'tp', None), P('tp'), P('tp', None), P('tp', None, None), P(None),
                P(None, 'tp', None, None), P('tp', None, None), P(None), P(None))
    out_specs = (row_spec, cache_spec, cache_spec, cache_spec)

    def local_step(hidden, cache_len, lin_state, k_cache, v_cache, norm_first, w_qkv, w_gate, slopes, out_norm,
                   w_out_lin, norm_second, w_attn, w_out_attn, mix_alpha, mix_beta):
        width = hidden.shape[1]
        dim = k_cache.shape[3]
        full_width = w_out_lin.shape[0] * dim * tp_size
        state_out, part, h1, tables, positions = lightning(hidden, cache_len, rotary_freq(dim), norm_first, w_qkv, w_gate, lin_state, slopes,
                                                out_norm, w_out_lin)
        h2, h2_own = all_reduce(functools.partial(finish_first, full_width), 0, tp_size, part,
                                (h1, norm_second.reshape(1, width), mix_alpha, mix_beta), [VMEM, VMEM, SMEM, SMEM],
                                width, "reduce_first")
        w_heads = w_attn.transpose(1, 2, 0, 3).reshape(w_attn.shape[2], width, dim)
        k_out, v_out, part = attention(cache_len, h2, w_heads, tables, positions, k_cache, v_cache,
                                       w_out_attn.reshape(w_out_attn.shape[0] * dim, width))
        hidden_out, _ = all_reduce(finish_second, 1, tp_size, part, (h2_own, mix_alpha, mix_beta), [VMEM, SMEM, SMEM],
                                   width, "reduce_second")
        return hidden_out, state_out, k_out, v_out

    return jax.shard_map(local_step, mesh=mesh, in_specs=in_specs, out_specs=out_specs, check_vma=False)
```

time: 123 us -> 88.6 us (0.72)
  Pallas kernels: 113 us -> 86.7 us
  local copies, waits for them, and re-layouts: 7.06 us -> 0.91 us
  other arithmetic: 1.58 us -> 0.01 us
    pallas_call x2, Pallas kernels: 66.6 us -> 40.2 us  [the longest x1 28.7 us: lightning(): pl.pallas_call(lightning_kernel, out_shape=(pltpu.HBM(lin_state.shape, f3...]
    unnamed x15 -> x23, local copies, waits for them, and re-layouts: 5.63 us -> 0.91 us
    reshape x1 -> x0, local copies, waits for them, and re-layouts: 1.27 us -> none  [lightning(): out_norm.reshape(heads, 1, dim)]
where the time goes in v2:
time: 88.6 us; the launch traced here: 88.5 us
  Pallas kernels  86.7 us (98%)
  local copies, waits for them, and re-layouts  0.91 us (1%)
    pallas_call x2, Pallas kernels, all_reduce(): pl.pallas_call(functools.partial(reduce_kernel, finish, chips, split, len...  46.5 us
    pallas_call x1, Pallas kernels, lightning(): pl.pallas_call(lightning_kernel, out_shape=(pltpu.HBM(lin_state.shape, f3...  28.7 us
    pallas_call x1, Pallas kernels, attention(): pl.pallas_call(attention_kernel, out_shape=(pltpu.HBM(k_cache.shape, k_ca...  11.5 us

profile of v2, /device:TPU:113, one launch (start us, length us, event | category | flops | bytes accessed | tf_op | source)
XLA Modules:
  0.0 88.5 jit_solution(15998291851529041962)
XLA Ops:
  0.6 0.0 copy-start.3
  0.6 0.0 copy-start.4
  0.7 0.0 copy-start.5
  0.7 0.0 slice-start
  0.7 0.0 slice-start.3
  0.7 28.7 %lightning.1 = (f32[64,5,128,128]{3,2,1,0:T(8,128)}, f32[8,8,5248]{2,1,0:T(8,128)S(1)}, f32[8,8,5120]{2,1,0:T(8,128)S(1)}, f32[3,64,128]{2,1,0:T(8,128)S(1)}, s32[64,8,128]{2,1,0:T(8,128)S(1)}) custom-call(f32[5]{0:T(128)} %slopes_hbm.1, s32[64]{0:T(128)} %len_ref.1, f32[1,128]{1,0:T(1,128)} %constant.2.clone.freq_hbm, f32[1,5120]{1,0:T(1,128)} %bitcast.17, ...), custom_call_target="tpu_custom_call" | custom-call | flops 2097152000 | bytes 74711040 | tf_op jit(solution)/shard_map/lightning/pallas_call | solution.py:166
  29.4 0.0 copy-done.3
  29.4 0.0 copy-done.4
  29.4 0.0 copy-done.5
  29.4 0.0 slice-start.1
  29.4 0.0 slice-start.2
  29.4 0.0 slice-start.4
  29.5 0.0 copy-start
  29.5 0.0 copy-start.1
  29.5 0.0 copy-start.2
  29.5 24.8 %reduce_first.1 = (bf16[64,5120]{1,0:T(8,128)(2,1)S(1)}, f32[8,5120]{1,0:T(8,128)S(1)}) custom-call(f32[8,8,5248]{2,1,0:T(8,128)S(1)} %get-tuple-element.15.part_ref, f32[8,8,5120]{2,1,0:T(8,128)S(1)} %get-tuple-element.16.refs_0_, f32[1,5120]{1,0:T(1,128)S(1)} %bitcast.14, f32[2]{0:T(128)S(1)} %copy-done.4, f32[2]{0:T(128)S(1)} %copy-done.5), custom_call_target="tpu_custom_call" | custom-call | flops 99999997952 | bytes 100000000 | tf_op jit(solution)/shard_map/reduce_first/pallas_call | solution.py:322
  54.3 0.0 slice-done
  54.3 0.0 slice-done.3
  54.3 0.0 slice-done.1
  54.3 0.0 slice-done.2
  54.3 0.0 slice-done.4
  54.4 11.5 %attention.1 = (bf16[64,1,512,128]{3,2,1,0:T(8,128)(2,1)}, bf16[64,1,512,128]{3,2,1,0:T(8,128)(2,1)}, f32[8,8,5120]{2,1,0:T(8,128)S(1)}) custom-call(s32[64]{0:T(128)S(1)} %copy-done.2, bf16[64,5120]{1,0:T(8,128)(2,1)S(1)} %get-tuple-element.17.h2_ref, f32[3,64,128]{2,1,0:T(8,128)S(1)} %get-tuple-element.18.table_ref, ...), custom_call_target="tpu_custom_call" | custom-call | flops 1174405120 | bytes 33554432 | tf_op jit(solution)/shard_map/attention/pallas_call | solution.py:460
  65.9 21.7 %reduce_second.1 = (bf16[64,5120]{1,0:T(8,128)(2,1)S(1)}, f32[8,5120]{1,0:T(8,128)}) custom-call(f32[8,8,5120]{2,1,0:T(8,128)S(1)} %get-tuple-element.20.part_ref, f32[8,5120]{1,0:T(8,128)S(1)} %get-tuple-element.21.refs_0_, f32[2]{0:T(128)S(1)} %copy-done.4, f32[2]{0:T(128)S(1)} %copy-done.5), custom_call_target="tpu_custom_call" | custom-call | flops 99999997952 | bytes 100000000 | tf_op jit(solution)/shard_map/reduce_second/pallas_call | solution.py:322
  87.6 0.8 copy.22
  (5 shorter events, 0.0 us)
Async XLA Ops:
  0.6 28.8 %copy-start.3 = (f32[5120]{0:T(1024)S(1)}, f32[5120]{0:T(1024)}, u32[]{:S(2)}) copy-start(f32[5120]{0:T(1024)} %param.28) | copy-start | bytes 61444
  0.6 28.8 %copy-start.4 = (f32[2]{0:T(128)S(1)}, f32[2]{0:T(128)}, u32[]{:S(2)}) copy-start(f32[2]{0:T(128)} %refs_1_.1) | copy-start | bytes 28
  0.7 28.8 %copy-start.5 = (f32[2]{0:T(128)S(1)}, f32[2]{0:T(128)}, u32[]{:S(2)}) copy-start(f32[2]{0:T(128)} %refs_2_.3) | copy-start | bytes 28
  0.7 53.6 %slice-start = ((s8[9175040]{0:T(1024)(128)(4,1)}), s8[4194304]{0:T(1024)(128)(4,1)S(1)}, s32[]{:S(2)}) async-start(s8[9175040]{0:T(1024)(128)(4,1)} %bitcast.8), calls=%async_computation | async-start | bytes 8388608
  0.7 53.6 %slice-start.3 = ((s8[8388608]{0:T(1024)(128)(4,1)}), s8[4194304]{0:T(1024)(128)(4,1)S(1)}, s32[]{:S(2)}) async-start(s8[8388608]{0:T(1024)(128)(4,1)} %bitcast.11), calls=%async_computation.3 | async-start | bytes 8388608
  29.4 24.9 %slice-start.1 = ((s8[9175040]{0:T(1024)(128)(4,1)}), s8[4194304]{0:T(1024)(128)(4,1)S(1)}, s32[]{:S(2)}) async-start(s8[9175040]{0:T(1024)(128)(4,1)} %bitcast.8), calls=%async_computation.1 | async-start | bytes 8388608
  29.4 24.9 %slice-start.2 = ((s8[9175040]{0:T(1024)(128)(4,1)}), s8[786432]{0:T(1024)(128)(4,1)S(1)}, s32[]{:S(2)}) async-start(s8[9175040]{0:T(1024)(128)(4,1)} %bitcast.8), calls=%async_computation.2 | async-start | bytes 1572864
  29.4 24.9 %slice-start.4 = ((s8[8388608]{0:T(1024)(128)(4,1)}), s8[4194304]{0:T(1024)(128)(4,1)S(1)}, s32[]{:S(2)}) async-start(s8[8388608]{0:T(1024)(128)(4,1)} %bitcast.11), calls=%async_computation.4 | async-start | bytes 8388608
  29.5 24.9 %copy-start = (bf16[64,1,512,128]{3,2,1,0:T(8,128)(2,1)S(1)}, bf16[64,1,512,128]{3,2,1,0:T(8,128)(2,1)}, u32[]{:S(2)}) copy-start(bf16[64,1,512,128]{3,2,1,0:T(8,128)(2,1)} %v_ref.1) | copy-start | bytes 25165828
  29.5 24.9 %copy-start.1 = (bf16[5,128,5120]{2,1,0:T(8,128)(2,1)S(1)}, bf16[5,128,5120]{2,1,0:T(8,128)(2,1)}, u32[]{:S(2)}) copy-start(bf16[5,128,5120]{2,1,0:T(8,128)(2,1)} %param.30) | copy-start | bytes 19660804
  29.5 24.9 %copy-start.2 = (s32[64]{0:T(128)S(1)}, s32[64]{0:T(128)}, u32[]{:S(2)}) copy-start(s32[64]{0:T(128)} %len_ref.1) | copy-start | bytes 772

commit v3 on v0

v3 whole, which is shorter than its diff:
```python
import functools

import jax
import jax.numpy as jnp
import numpy as np
from jax import lax
from jax.experimental import pallas as pl
from jax.experimental.pallas import tpu as pltpu
from jax.sharding import PartitionSpec as P

EPS = 1e-5
ROPE_BASE = 10000000.0
MESH = pl.DeviceIdType.MESH
VMEM = pl.BlockSpec(memory_space=pltpu.VMEM)
SMEM = pl.BlockSpec(memory_space=pltpu.SMEM)
HBM = pl.BlockSpec(memory_space=pltpu.HBM)
ROWS = 8
LANES = 128
VMEM_LIMIT = 155 << 16


class Ring:
    def __init__(self, chips, send_sem, recv_sem):
        me = lax.axis_index("tp")
        self.me, chip, self.core = me, me // 2, me % 2
        self.order = ((chip + 2) % chips, (chip + 1) % chips, (chip + chips - 1) % chips, chip)
        self.mate = 2 * chip + (1 - self.core)
        self.up, self.down = 2 * self.order[1] + self.core, 2 * self.order[2] + self.core
        self.send_sem, self.recv_sem = send_sem, recv_sem
        self.copies = []

    def signal(self):
        for peer in (self.mate, self.up, self.down):
            pl.semaphore_signal(pltpu.get_barrier_semaphore(), inc=1, device_id={"tp": peer}, device_id_type=MESH)

    def wait(self):
        pl.semaphore_wait(pltpu.get_barrier_semaphore(), 3)

    def send(self, src, dst, peer):
        i = len(self.copies)
        c = pltpu.make_async_remote_copy(src_ref=src, dst_ref=dst, send_sem=self.send_sem.at[i], recv_sem=self.recv_sem.at[i],
                                         device_id={"tp": peer}, device_id_type=MESH)
        c.start()
        self.copies.append(c)
        return c

    def drain(self):
        for c in self.copies:
            c.wait_send()


class RowSum:
    def __init__(self, ring, split, part_ref, pair_ref, acc_ref, landing):
        self.ring, self.part, self.pair, self.acc, self.landing = ring, part_ref, pair_ref, acc_ref, landing
        width = part_ref.shape[2]
        self.lo, self.hi = pl.ds(0, split), pl.ds(split, width - split)
        self.mates = []

    def to_mate(self, s):
        t = self.ring.order[s]
        self.mates.append(self.ring.send(self.part.at[2 * t + (1 - self.ring.core)], self.pair.at[s], self.ring.mate))

    def add_mate(self, s):
        self.mates[s].wait_recv()
        self.acc[s] = self.part[2 * self.ring.order[s] + self.ring.core] + self.pair[s]

    def far(self):
        self.add_mate(0)
        self.far_up = self.ring.send(self.acc.at[0, :, self.lo], self.landing[0], self.ring.up)
        self.far_down = self.ring.send(self.acc.at[0, :, self.hi], self.landing[1], self.ring.down)

    def next(self):
        self.add_mate(1)
        self.near_up = self.ring.send(self.acc.at[1, :, self.hi], self.landing[2], self.ring.up)

    def previous(self):
        self.add_mate(2)
        self.near_down = self.ring.send(self.acc.at[2, :, self.lo], self.landing[3], self.ring.down)

    def relay(self):
        self.far_up.wait_recv()
        self.acc[1, :, self.lo] += self.landing[0][...]
        self.sum_up = self.ring.send(self.acc.at[1, :, self.lo], self.landing[4], self.ring.up)
        self.far_down.wait_recv()
        self.acc[2, :, self.hi] += self.landing[1][...]
        self.sum_down = self.ring.send(self.acc.at[2, :, self.hi], self.landing[5], self.ring.down)

    def own(self):
        self.add_mate(3)
        self.near_up.wait_recv()
        self.acc[3, :, self.hi] += self.landing[2][...]
        self.near_down.wait_recv()
        self.acc[3, :, self.lo] += self.landing[3][...]
        self.sum_up.wait_recv()
        self.acc[3, :, self.lo] += self.landing[4][...]
        self.sum_down.wait_recv()
        self.acc[3, :, self.hi] += self.landing[5][...]

    @staticmethod
    def scratch(chips, rows, width, split):
        f32 = jnp.float32
        halves = [pltpu.VMEM((rows, n), f32) for n in (split, width - split, width - split, split, split, width - split)]
        return [pltpu.VMEM((chips, rows, width), f32), pltpu.VMEM((chips, rows, width), f32)] + halves


def gather_rows(ring, gather_ref):
    out_width = gather_ref.shape[2]
    cut = out_width // 2
    first, second = pl.ds(0, cut), pl.ds(cut, out_width - cut)
    me, up, down, mate = ring.me, ring.up, ring.down, ring.mate
    far = 2 * ring.order[0] + ring.core

    def move(dev, cols, peer):
        return ring.send(gather_ref.at[dev, :, cols], gather_ref.at[dev, :, cols], peer)

    up_first, down_second = move(me, first, up), move(me, second, down)
    up_second, down_first = move(me, second, up), move(me, first, down)
    arrivals = [move(me, pl.ds(0, out_width), mate)]
    up_first.wait_recv()
    relay_up = move(down, first, up)
    arrivals.append(move(down, first, mate))
    down_second.wait_recv()
    relay_down = move(up, second, down)
    arrivals.append(move(up, second, mate))
    up_second.wait_recv()
    arrivals.append(move(down, second, mate))
    down_first.wait_recv()
    arrivals.append(move(up, first, mate))
    relay_up.wait_recv()
    arrivals.append(move(far, first, mate))
    relay_down.wait_recv()
    arrivals.append(move(far, second, mate))
    for c in arrivals:
        c.wait_recv()


def half_of(width):
    return (width // LANES + 1) // 2 * LANES


def second_kernel(chips, part_ref, h2_ref, alpha_ref, beta_ref, out_ref, pair_ref, acc_ref, *refs):
    landing, (gather_ref, send_sem, recv_sem) = refs[:6], refs[6:]
    ring = Ring(chips, send_sem, recv_sem)
    total = RowSum(ring, half_of(part_ref.shape[2]), part_ref, pair_ref, acc_ref, landing)
    ring.signal()
    ring.wait()
    for s in range(4):
        total.to_mate(s)
    total.far()
    total.next()
    total.previous()
    total.relay()
    total.own()
    out = alpha_ref[1] * h2_ref[...] + beta_ref[1] * acc_ref[3]
    gather_ref[ring.me] = out.astype(jnp.bfloat16).astype(jnp.float32)
    gather_rows(ring, gather_ref)
    out_ref[...] = gather_ref[...].reshape(out_ref.shape).astype(out_ref.dtype)
    ring.drain()


def second_sum(tp_size, part, h2_own, mix_alpha, mix_beta):
    blocks, rows, width = part.shape
    chips = tp_size // 2
    return pl.pallas_call(
        functools.partial(second_kernel, chips),
        out_shape=jax.ShapeDtypeStruct((blocks * rows, width), jnp.bfloat16),
        in_specs=[VMEM, VMEM, SMEM, SMEM],
        out_specs=VMEM,
        scratch_shapes=RowSum.scratch(chips, rows, width, half_of(width)) + [
            pltpu.VMEM((blocks, rows, width), jnp.float32),
            pltpu.SemaphoreType.DMA((32,)), pltpu.SemaphoreType.DMA((32,)),
        ],
        compiler_params=pltpu.CompilerParams(collective_id=1, has_side_effects=True, vmem_limit_bytes=VMEM_LIMIT),
        cost_estimate=pl.CostEstimate(flops=10 ** 11, transcendentals=0, bytes_accessed=10 ** 8),
        name="second_sum",
    )(part, h2_own, mix_alpha, mix_beta)


def first_kernel(chips, full_width,
                 slopes_hbm, len_hbm, freq_hbm, norm_hbm, onorm_hbm, norm2_hbm, alpha_hbm, beta_hbm, hidden_hbm,
                 wqkv_hbm, wgate_hbm, state_hbm, wout_hbm, watt_hbm, wout2_hbm, k_hbm, v_hbm,
                 state_ref, watt_ref, wout_ref, k_ref, v_ref, h2_ref, own_ref, table_ref, pos_ref,
                 slopes_ref, len_ref, freq_ref, norm_ref, onorm_ref, norm2_ref, alpha_ref, beta_ref,
                 h1_ref, proj_ref, o_ref, part_ref, gather_ref, small_sem, w_sem, wout_sem, state_sem, late_sem, send_sem, recv_sem,
                 pair_ref, acc_ref, *landing):
    batch, width = h2_ref.shape
    heads, dim = onorm_ref.shape
    slots = watt_ref.shape[0]
    blocks = batch // ROWS
    ring = Ring(chips, send_sem, recv_sem)
    total = RowSum(ring, half_of(part_ref.shape[2]), part_ref, pair_ref, acc_ref, landing)

    def piece(h, j):
        slot = (4 * h + j) % slots
        src = wqkv_hbm.at[j, h] if j < 3 else wgate_hbm.at[h]
        return pltpu.make_async_copy(src, watt_ref.at[slot], w_sem.at[slot])

    def wout_copy(h):
        return pltpu.make_async_copy(wout_hbm.at[h], wout_ref.at[h], wout_sem.at[h])

    def state_copy(s, half):
        rows = pl.ds(2 * ROWS * ring.order[s] + half * ROWS, ROWS)
        return pltpu.make_async_copy(state_hbm.at[rows], state_ref.at[rows], state_sem.at[s, half])

    small = [pltpu.make_async_copy(src, dst, small_sem.at[i])
             for i, (src, dst) in enumerate(((len_hbm, len_ref), (freq_hbm, freq_ref), (hidden_hbm, h2_ref), (norm_hbm, norm_ref),
                                             (slopes_hbm, slopes_ref), (onorm_hbm, onorm_ref), (norm2_hbm, norm2_ref),
                                             (alpha_hbm, alpha_ref), (beta_hbm, beta_ref)))]
    for c in small:
        c.start()
    for n in range(slots):
        piece(n // 4, n % 4).start()
    for c in small[:2]:
        c.wait()
    for r in range(batch):
        pos_ref[r] = jnp.full((ROWS, LANES), len_ref[r], jnp.int32)
    angle = pos_ref[:, 0, :].astype(jnp.float32) * freq_ref[...]
    cosine, sine = jnp.cos(angle), jnp.sin(angle)
    lane = lax.broadcasted_iota(jnp.int32, angle.shape, 1)
    table_ref[0] = jnp.where(lane < dim // 2, cosine, 1.0)
    table_ref[1] = jnp.where(lane < dim // 4, -sine, 0.0)
    table_ref[2] = jnp.where((lane >= dim // 4) & (lane < dim // 2), sine, 0.0)

    for c in small[2:]:
        c.wait()
    x = h2_ref[...].astype(jnp.float32)
    h1 = x * lax.rsqrt(jnp.mean(x * x, axis=-1, keepdims=True) + EPS) * norm_ref[...]
    h1 = h1.astype(jnp.bfloat16)
    h1_ref[...] = h1
    gather_ref[...] = h1.astype(jnp.float32).reshape(gather_ref.shape)
    ring.signal()

    def one_head(h, _):
        for j in range(4):
            piece(h, j).wait()
            y = jnp.dot(h1_ref[...], watt_ref[(4 * h + j) % slots], preferred_element_type=jnp.float32)
            gate = jax.nn.sigmoid(y)
            proj_ref[j, h] = gate if j == 3 else (y * gate).astype(jnp.bfloat16).astype(jnp.float32)
            ahead, later = (j + slots) // 4, (j + slots) % 4

            @pl.when(h + ahead < heads)
            def _():
                piece(h + ahead, later).start()

            @pl.when(h == heads - 2)
            def _():
                if j == 1:
                    for i in range(heads // 2):
                        wout_copy(i).start()
                if j >= 2:
                    state_copy(0, j - 2).start()

            @pl.when(h == heads - 1)
            def _():
                if j == 0:
                    for i in range(heads // 2, heads):
                        wout_copy(i).start()
                if j >= 2:
                    state_copy(1, j - 2).start()
        return 0

    lax.fori_loop(0, heads, one_head, 0)
    ring.wait()

    late = [pltpu.make_async_copy(watt_hbm.at[j], watt_ref.at[j], late_sem.at[0, j]) for j in range(slots)]
    caches = [pltpu.make_async_copy(src.at[pl.ds(i * 16, 16)], dst.at[pl.ds(i * 16, 16)], late_sem.at[1 + which, i])
              for which, (src, dst) in enumerate(((k_hbm, k_ref), (v_hbm, v_ref))) for i in range(batch // 16)]
    wout2 = [pltpu.make_async_copy(wout2_hbm.at[h], wout_ref.at[h], late_sem.at[3, h]) for h in range(heads)]

    pair_rows = 2 * ROWS
    wide = ROWS * dim
    row_id = lax.broadcasted_iota(jnp.int32, (pair_rows, wide), 0)
    lane_block = lax.broadcasted_iota(jnp.int32, (pair_rows, wide), 1) // dim
    contract = (((0,), (0,)), ((), ()))

    def update(base):
        def body(h, _):
            decay = jnp.exp(-jnp.full((1, dim), slopes_ref[h], jnp.float32))
            rows = pl.ds(base, pair_rows)
            q = proj_ref[0, h, rows, :].astype(jnp.bfloat16)
            k = proj_ref[1, h, rows, :].astype(jnp.bfloat16)
            v = jnp.concatenate([proj_ref[2, h, rows, :]] * ROWS, axis=1)
            for half in range(2):
                mine = lane_block + half * ROWS == row_id
                spread_v = jnp.where(mine, v, 0.0).astype(jnp.bfloat16)
                ones = jnp.where(mine, 1.0, 0.0).astype(jnp.bfloat16)
                outer = lax.dot_general(k, spread_v, contract, preferred_element_type=jnp.float32)
                q_all = lax.dot_general(q, ones, contract, preferred_element_type=jnp.float32)
                outs = []
                for r in range(ROWS):
                    row = base + half * ROWS + r
                    cols = slice(r * dim, (r + 1) * dim)
                    new = decay * state_ref[row, h] + outer[:, cols]
                    state_ref[row, h] = new
                    outs.append(jnp.sum(q_all[:, cols] * new, axis=0, keepdims=True))
                o_ref[h, pl.ds(half * ROWS, ROWS), :] = jnp.concatenate(outs, axis=0)
            return 0

        lax.fori_loop(0, heads, body, 0)

    def project_out(t, base):
        squares = jnp.zeros((pair_rows, 1), jnp.float32)
        gated = []
        for h in range(heads):
            o = o_ref[h]
            squares += jnp.sum(o * o, axis=1, keepdims=True)
            gated.append((o * onorm_ref[h:h + 1, :] * proj_ref[3, h, pl.ds(base, pair_rows), :]).astype(jnp.bfloat16))
        gated = jnp.concatenate(gated, axis=1)
        tile = 1024
        for c in range(width // tile):
            cols = pl.ds(c * tile, tile)
            w = wout_ref[:, :, cols].reshape(heads * dim, tile)
            y = jnp.dot(gated, w, preferred_element_type=jnp.float32)
            part_ref[pl.ds(2 * t, 2), :, cols] = y.reshape(2, ROWS, tile)
        part_ref[pl.ds(2 * t, 2), :, pl.ds(width, LANES)] = jnp.broadcast_to(squares, (pair_rows, LANES)).reshape(2, ROWS, LANES)

    for s in range(4):
        t = ring.order[s]
        base = pl.multiple_of(t * pair_rows, pair_rows)
        for c in [state_copy(s + 2, 0), state_copy(s + 2, 1)] if s < 2 else (late, caches)[s - 2]:
            c.start()
        for half in range(2):
            state_copy(s, half).wait()
        update(base)
        if s == 0:
            for h in range(heads):
                wout_copy(h).wait()
        if s == 3:
            total.previous()
            total.relay()
        project_out(t, base)
        total.to_mate(s)
        if s == 1:
            total.far()
        if s == 2:
            total.next()
    for c in wout2:
        c.start()
    total.own()

    inv = lax.rsqrt(acc_ref[3, :, pl.ds(width, 1)] / full_width + EPS)
    lin = acc_ref[3, :, pl.ds(0, width)] * inv
    mid = (alpha_ref[0] * gather_ref[ring.me] + beta_ref[0] * lin).astype(jnp.bfloat16).astype(jnp.float32)
    h2 = mid * lax.rsqrt(jnp.mean(mid * mid, axis=-1, keepdims=True) + EPS) * norm2_ref[...]
    h2 = h2.astype(jnp.bfloat16).astype(jnp.float32)
    own_ref[...] = h2
    gather_ref[ring.me] = h2
    gather_rows(ring, gather_ref)
    h2_ref[...] = gather_ref[...].reshape(h2_ref.shape).astype(h2_ref.dtype)
    ring.drain()
    for c in late + caches + wout2:
        c.wait()


def in_hbm(x):
    return pltpu.with_memory_space_constraint(x, pltpu.HBM)


def in_vmem(x):
    return pltpu.with_memory_space_constraint(x, pltpu.VMEM)


def first_sublayer(tp_size, slopes, cache_len, freq, norm_first, out_norm, norm_second, mix_alpha, mix_beta, hidden,
                   w_qkv, w_gate, lin_state, w_out_lin, w_attn, w_out_attn, k_cache, v_cache):
    batch, width = hidden.shape
    heads, dim = out_norm.shape
    blocks = batch // ROWS
    slots = w_attn.shape[0]
    chips = tp_size // 2
    f32, bf16 = jnp.float32, jnp.bfloat16
    part_width = width + LANES
    args = (slopes, cache_len, freq, norm_first.reshape(1, width), out_norm, norm_second.reshape(1, width), mix_alpha, mix_beta, hidden,
            w_qkv, w_gate, lin_state, w_out_lin, w_attn, w_out_attn, k_cache, v_cache)
    dma = pltpu.SemaphoreType.DMA
    return pl.pallas_call(
        functools.partial(first_kernel, chips, heads * dim * tp_size),
        out_shape=(pltpu.VMEM(lin_state.shape, f32),
                   pltpu.VMEM((slots, width, dim), bf16),
                   pltpu.VMEM((heads, dim, width), bf16),
                   pltpu.VMEM(k_cache.shape, k_cache.dtype),
                   pltpu.VMEM(v_cache.shape, v_cache.dtype),
                   pltpu.VMEM((batch, width), bf16),
                   pltpu.VMEM((ROWS, width), f32),
                   pltpu.VMEM((3, batch, dim), f32),
                   pltpu.VMEM((batch, ROWS, LANES), jnp.int32)),
        in_specs=[HBM] * len(args),
        out_specs=(VMEM,) * 9,
        scratch_shapes=[
            pltpu.SMEM((heads,), f32), pltpu.SMEM((batch,), jnp.int32), pltpu.VMEM((1, dim), f32), pltpu.VMEM((1, width), f32),
            pltpu.VMEM((heads, dim), f32), pltpu.VMEM((1, width), f32), pltpu.SMEM((2,), f32), pltpu.SMEM((2,), f32),
            pltpu.VMEM((batch, width), bf16),
            pltpu.VMEM((4, heads, batch, dim), f32),
            pltpu.VMEM((heads, 2 * ROWS, dim), f32),
            pltpu.VMEM((blocks, ROWS, part_width), f32),
            pltpu.VMEM((blocks, ROWS, width), f32),
            dma((9,)), dma((slots,)), dma((heads,)), dma((4, 2)), dma((4, 8)), dma((32,)), dma((32,)),
        ] + RowSum.scratch(chips, ROWS, part_width, half_of(part_width)),
        compiler_params=pltpu.CompilerParams(collective_id=0, has_side_effects=True, vmem_limit_bytes=VMEM_LIMIT),
        cost_estimate=pl.CostEstimate(flops=10 ** 11, transcendentals=0, bytes_accessed=10 ** 8),
        name="first_sublayer",
    )(*[in_hbm(x) for x in args])


def attention_kernel(len_ref, h2_ref, table_ref, pos_ref, watt_ref, k_ref, v_ref, wout_ref, state_ref,
                     k_out_hbm, v_out_hbm, state_out_hbm, part_ref, q_ref, kn_ref, vn_ref, att_ref, patch_ref, bulk_sem, patch_sem,
                     state_sem):
    batch, width = h2_ref.shape
    group = watt_ref.shape[0] - 2
    dim = watt_ref.shape[2]
    tmax = k_ref.shape[2]
    per = 8
    sub = 16
    blocks = batch // per

    def bulk(i, which):
        src, dst = ((k_ref, k_out_hbm), (v_ref, v_out_hbm))[which]
        rows = pl.ds(i * per, per)
        return pltpu.make_async_copy(src.at[rows], dst.at[rows], bulk_sem.at[i, which])

    def patch(b, which):
        dst = (k_out_hbm, v_out_hbm)[which]
        start = pl.multiple_of((len_ref[b] // sub) * sub, sub)
        return pltpu.make_async_copy(patch_ref.at[which, b], dst.at[b, 0, pl.ds(start, sub)], patch_sem.at[b, which])

    for i in range(blocks):
        for which in range(2):
            bulk(i, which).start()
    states = [pltpu.make_async_copy(state_ref.at[pl.ds(i * per, per)], state_out_hbm.at[pl.ds(i * per, per)], state_sem.at[i])
              for i in range(blocks)]
    for c in states:
        c.start()

    h2 = h2_ref[...]

    def turn(x):
        return (x * table_ref[0] + pltpu.roll(x, dim - dim // 4, 1) * table_ref[1] + pltpu.roll(x, dim // 4, 1) * table_ref[2])

    q_ref[...] = jnp.zeros_like(q_ref)
    for j in range(group):
        q_ref[:, j, :] = turn(jnp.dot(h2, watt_ref[j], preferred_element_type=jnp.float32))
    kn_ref[...] = turn(jnp.dot(h2, watt_ref[group], preferred_element_type=jnp.float32)).astype(jnp.bfloat16).astype(jnp.float32)
    vn_ref[...] = jnp.dot(h2, watt_ref[group + 1], preferred_element_type=jnp.float32).astype(jnp.bfloat16).astype(jnp.float32)

    rows16 = lax.broadcasted_iota(jnp.int32, (sub, dim), 0)
    flat = per * ROWS
    cols = lax.broadcasted_iota(jnp.int32, (flat, tmax), 1)
    scale = dim ** -0.5

    def spread(rows):
        return jnp.concatenate([jnp.broadcast_to(rows[r:r + 1, :], (ROWS, dim)) for r in range(per)], axis=0)

    def block(i, _):
        base = pl.multiple_of(i * per, per)
        news = [kn_ref[pl.ds(base, per), :], vn_ref[pl.ds(base, per), :]]
        for r in range(per):
            b = base + r
            pos = len_ref[b]
            start = pl.multiple_of((pos // sub) * sub, sub)
            for which, ref in ((0, k_ref), (1, v_ref)):
                old = ref[b, 0, pl.ds(start, sub), :].astype(jnp.float32)
                patch_ref[which, b] = jnp.where(rows16 == pos - start, news[which][r:r + 1, :], old).astype(jnp.bfloat16)
        q = q_ref[pl.ds(base, per)].reshape(flat, dim)
        q_bf = q.astype(jnp.bfloat16)
        s_new = jnp.sum(q_bf.astype(jnp.float32) * spread(news[0]), axis=1, keepdims=True)
        scores = [lax.dot_general(q_bf[r * ROWS:(r + 1) * ROWS], k_ref[base + r, 0], (((1,), (1,)), ((), ())),
                                  preferred_element_type=jnp.float32) for r in range(per)]
        s = jnp.concatenate(scores, axis=0)
        pos = pos_ref[pl.ds(base, per)].reshape(flat, LANES)
        pos = jnp.concatenate([pos] * (tmax // LANES), axis=1)
        at_pos = cols == pos
        s = jnp.where(at_pos, s_new, s) * scale
        s = jnp.where(cols <= pos, s, -jnp.inf)
        e = jnp.exp(s - jnp.max(s, axis=1, keepdims=True))
        p = (e * (1.0 / jnp.sum(e, axis=1, keepdims=True))).astype(jnp.bfloat16).astype(jnp.float32)
        p_new = jnp.sum(jnp.where(at_pos, p, 0.0), axis=1, keepdims=True)
        p_old = jnp.where(at_pos, 0.0, p).astype(jnp.bfloat16)
        outs = [jnp.dot(p_old[r * ROWS:(r + 1) * ROWS], v_ref[base + r, 0], preferred_element_type=jnp.float32)
                for r in range(per)]
        att = jnp.concatenate(outs, axis=0) + p_new * spread(news[1])
        att_ref[pl.ds(base, per)] = att.reshape(per, ROWS, dim)
        for which in range(2):
            bulk(i, which).wait()
        for r in range(per):
            for which in range(2):
                patch(base + r, which).start()
        return 0

    lax.fori_loop(0, blocks, block, 0)
    rows = jnp.concatenate([att_ref[:, j, :] for j in range(group)], axis=1).astype(jnp.bfloat16)
    tile = 1024
    for c in range(width // tile):
        cs = pl.ds(c * tile, tile)
        piece = jnp.dot(rows, wout_ref[:, :, cs].reshape(group * dim, tile), preferred_element_type=jnp.float32)
        part_ref[:, :, cs] = piece.reshape(batch // ROWS, ROWS, tile)

    def finish(b, _):
        for which in range(2):
            patch(b, which).wait()
        return 0

    lax.fori_loop(0, batch, finish, 0)
    for c in states:
        c.wait()


def attention(cache_len, h2, w_attn, tables, positions, k_cache, v_cache, w_out, state):
    batch, width = h2.shape
    _, _, tmax, dim = k_cache.shape
    slots = w_attn.shape[0]
    blocks = batch // ROWS
    return pl.pallas_call(
        attention_kernel,
        out_shape=(pltpu.HBM(k_cache.shape, k_cache.dtype), pltpu.HBM(v_cache.shape, v_cache.dtype),
                   pltpu.HBM(state.shape, state.dtype),
                   pltpu.VMEM((blocks, ROWS, width), jnp.float32)),
        in_specs=[SMEM] + [VMEM] * 8,
        out_specs=(HBM, HBM, HBM, VMEM),
        scratch_shapes=[
            pltpu.VMEM((batch, ROWS, dim), jnp.float32),
            pltpu.VMEM((batch, dim), jnp.float32),
            pltpu.VMEM((batch, dim), jnp.float32),
            pltpu.VMEM((batch, ROWS, dim), jnp.float32),
            pltpu.VMEM((2, batch, 16, dim), k_cache.dtype),
            pltpu.SemaphoreType.DMA((batch // 8, 2)),
            pltpu.SemaphoreType.DMA((batch, 2)),
            pltpu.SemaphoreType.DMA((batch // 8,)),
        ],
        compiler_params=pltpu.CompilerParams(vmem_limit_bytes=VMEM_LIMIT),
        cost_estimate=pl.CostEstimate(flops=2 * batch * width * dim * slots * 2, transcendentals=0,
                                      bytes_accessed=4 * k_cache.size * 2),
        name="attention",
    )(cache_len, *[in_vmem(x) for x in (h2, tables, positions, w_attn, k_cache, v_cache, w_out, state)])


def rotary_freq(dim):
    rot = dim // 2
    half = rot // 2
    freq = ROPE_BASE ** (-2.0 * np.arange(half) / rot)
    return jnp.asarray(np.concatenate([freq, freq, np.zeros(dim - rot)])[None, :], jnp.float32)


def solution(mesh):
    tp_size = mesh.shape['tp']
    row_spec = P('dp', None)
    cache_spec = P('dp', 'tp', None, None)
    in_specs = (row_spec, P('dp'), cache_spec, cache_spec, cache_spec, P(None), P(None, None, 'tp', None),
                P(None, 'tp', None), P('tp'), P('tp', None), P('tp', None, None), P(None),
                P(None, 'tp', None, None), P('tp', None, None), P(None), P(None))
    out_specs = (row_spec, cache_spec, cache_spec, cache_spec)

    def local_step(hidden, cache_len, lin_state, k_cache, v_cache, norm_first, w_qkv, w_gate, slopes, out_norm,
                   w_out_lin, norm_second, w_attn, w_out_attn, mix_alpha, mix_beta):
        width = hidden.shape[1]
        dim = k_cache.shape[3]
        w_heads = w_attn.transpose(1, 2, 0, 3).reshape(w_attn.shape[2], width, dim)
        state, w_heads, w_out, keys, values, h2, h2_own, tables, positions = first_sublayer(
            tp_size, slopes, cache_len, rotary_freq(dim), norm_first, out_norm, norm_second, mix_alpha, mix_beta, hidden,
            w_qkv.transpose(1, 2, 0, 3), w_gate.transpose(1, 0, 2), lin_state, w_out_lin, w_heads, w_out_attn, k_cache, v_cache)
        k_out, v_out, state_out, part = attention(cache_len, h2, w_heads, tables, positions, keys, values, w_out, state)
        hidden_out = second_sum(tp_size, part, h2_own, mix_alpha, mix_beta)
        return hidden_out, state_out, k_out, v_out

    return jax.shard_map(local_step, mesh=mesh, in_specs=in_specs, out_specs=out_specs, check_vma=False)
```

time: 216 us -> 80.5 us (0.37); the launches traced: 214 us -> 80.5 us
  waiting for transfers between devices: 108 us -> 0 us
  Pallas kernels: 0 us -> 78.9 us
  matrix products: 45.9 us -> 0 us
  other arithmetic: 28.9 us -> 0 us
  between operations: 14.3 us -> 0.69 us
  blocking collectives: 13.6 us -> 0 us
    psum x2 -> x0, waiting for transfers between devices: 108 us -> none  [the longest x1 54.5 us: local_step(): attn_out = lax.psum(attn_part, 'tp')]
    pallas_call x0 -> x3, Pallas kernels: none -> 78.9 us  [the longest x1 43 us: first_sublayer(): pl.pallas_call(functools.partial(first_kernel, chips, heads * dim * tp_si...]
    dot_general x7 -> x0, matrix products: 45.9 us -> none  [the longest x1 10.4 us: local_step(): jnp.einsum('bd,dchk->bchk', h_first, w_qkv, preferred_element_type=jnp.fl...]
    psum x1 -> x0, blocking collectives: 13.6 us -> none  [local_step(): sq_sum = lax.psum(jnp.sum(lin_attn * lin_attn, axis=(1, 2)), 'tp')]
    select_n x1 -> x0, other arithmetic: 9.47 us -> none  [local_step(): k_out = jnp.where(write_mask, key_new, k_cache)]
    add x1 -> x0, other arithmetic: 9.46 us -> none  [local_step(): decay_rate * lin_state]
    reduce_sum x3 -> x0, other arithmetic: 4.56 us -> none  [the longest x2 4.45 us: rms_scale(): jnp.mean(wide_vals * wide_vals, axis=-1, keepdims=True) + EPS]
    convert_element_type x2 -> x0, other arithmetic: 3.73 us -> none  [the longest x1 3.73 us: local_step(): (mix_alpha[1] * h_second.astype(jnp.float32) + mix_beta[1] * attn_out).as...]
  transfers between devices with their start and end apart: 2 -> 0, of which waited for: 2 -> 0; matrix products, arithmetic and copies ran while one was open for 1% -> 0% of each run, Pallas kernels for 0% -> 0%
where the time goes in v3:
time: 80.5 us
  Pallas kernels  78.9 us (98%)
  local copies, waits for them, and re-layouts  0.85 us (1%)
    pallas_call x1, Pallas kernels, first_sublayer(): pl.pallas_call(functools.partial(first_kernel, chips, heads * dim * tp_si...  43 us
    pallas_call x1, Pallas kernels, second_sum(): pl.pallas_call(functools.partial(second_kernel, chips), out_shape=jax.Sha...  20.6 us
    pallas_call x1, Pallas kernels, attention(): pl.pallas_call(attention_kernel, out_shape=(pltpu.HBM(k_cache.shape, k_ca...  15.3 us

profile of v3, /device:TPU:113, one launch (start us, length us, event | category | flops | bytes accessed | tf_op | source)
XLA Modules:
  0.0 80.5 jit_solution(9810529543697079645)
XLA Ops:
  0.6 43.0 %first_sublayer.1 = (f32[64,5,128,128]{3,2,1,0:T(8,128)S(1)}, bf16[7,5120,128]{2,1,0:T(8,128)(2,1)S(1)}, bf16[5,128,5120]{2,1,0:T(8,128)(2,1)S(1)}, bf16[64,1,51...) custom-call(f32[5]{0:T(128)} %slopes_hbm.1, ...), custom_call_target="tpu_custom_call" | custom-call | flops 99999997952 | bytes 100000000 | tf_op jit(solution)/shard_map/first_sublayer/pallas_call | solution.py:375
  43.6 0.0 copy-start
  43.7 0.0 copy-start.1
  43.7 15.3 %attention.1 = (bf16[64,1,512,128]{3,2,1,0:T(8,128)(2,1)}, bf16[64,1,512,128]{3,2,1,0:T(8,128)(2,1)}, f32[64,5,128,128]{3,2,1,0:T(8,128)}, f32[8,8,5120]{2,1,0:T(8,128)S(1)}) custom-call(s32[64]{0:T(128)} %len_ref.1, bf16[64,5120]{1,0:T(8,128)(2,1)S(1)} %get-tuple-element.17.h2_ref, f32[3,64,128]{2,1,0:T(8,128)S(1)} %get-tuple-element.18.table_ref, ...), custom_call_target="tpu_custom_call" | custom-call | flops 1174405120 | bytes 33554432 | tf_op jit(solution)/shard_map/attention/pallas_call | solution.py:511
  59.0 0.0 copy-done
  59.0 0.0 copy-done.1
  59.0 20.6 %second_sum.1 = bf16[64,5120]{1,0:T(8,128)(2,1)S(1)} custom-call(f32[8,8,5120]{2,1,0:T(8,128)S(1)} %get-tuple-element.25.part_ref, f32[8,5120]{1,0:T(8,128)S(1)} %get-tuple-element.26.h2_ref, f32[2]{0:T(128)S(1)} %copy-done, f32[2]{0:T(128)S(1)} %copy-done.1), custom_call_target="tpu_custom_call" | custom-call | flops 99999997952 | bytes 100000000 | tf_op jit(solution)/shard_map/second_sum/pallas_call | solution.py:164
  79.6 0.8 %copy.22 = bf16[64,5120]{1,0:T(8,128)(2,1)} copy(bf16[64,5120]{1,0:T(8,128)(2,1)S(1)} %second_sum.1) | data formatting | bytes 1310720
Async XLA Ops:
  43.6 15.3 %copy-start = (f32[2]{0:T(128)S(1)}, f32[2]{0:T(128)}, u32[]{:S(2)}) copy-start(f32[2]{0:T(128)} %alpha_ref.1) | copy-start | bytes 28
  43.7 15.3 %copy-start.1 = (f32[2]{0:T(128)S(1)}, f32[2]{0:T(128)}, u32[]{:S(2)}) copy-start(f32[2]{0:T(128)} %beta_ref.1) | copy-start | bytes 28

commit v4 on v3

--- a/solution.py
+++ b/solution.py
@@ -325,15 +325,15 @@
         if s == 0:
             for h in range(heads):
                 wout_copy(h).wait()
+        if s == 1:
+            total.far()
+        if s == 2:
+            total.next()
         if s == 3:
             total.previous()
             total.relay()
         project_out(t, base)
         total.to_mate(s)
-        if s == 1:
-            total.far()
-        if s == 2:
-            total.next()
     for c in wout2:
         c.start()
     total.own()

time: 80.5 us -> 80.5 us (level)
  no operation moved by 1% of the time
where the time goes in v4:
time: 80.5 us; the launch traced here: 80.4 us
  Pallas kernels  78.8 us (98%)
  local copies, waits for them, and re-layouts  0.85 us (1%)
    pallas_call x1, Pallas kernels, first_sublayer(): pl.pallas_call(functools.partial(first_kernel, chips, heads * dim * tp_si...  42.9 us
    pallas_call x1, Pallas kernels, second_sum(): pl.pallas_call(functools.partial(second_kernel, chips), out_shape=jax.Sha...  20.6 us
    pallas_call x1, Pallas kernels, attention(): pl.pallas_call(attention_kernel, out_shape=(pltpu.HBM(k_cache.shape, k_ca...  15.3 us

profile of v4, /device:TPU:113, one launch (start us, length us, event | category | flops | bytes accessed | tf_op | source)
XLA Modules:
  0.0 80.4 jit_solution(14467031689225427956)
XLA Ops:
  0.6 42.9 %first_sublayer.1 = (f32[64,5,128,128]{3,2,1,0:T(8,128)S(1)}, bf16[7,5120,128]{2,1,0:T(8,128)(2,1)S(1)}, bf16[5,128,5120]{2,1,0:T(8,128)(2,1)S(1)}, bf16[64,1,51...) custom-call(f32[5]{0:T(128)} %slopes_hbm.1, ...), custom_call_target="tpu_custom_call" | custom-call | flops 99999997952 | bytes 100000000 | tf_op jit(solution)/shard_map/first_sublayer/pallas_call | solution.py:375
  43.6 0.0 copy-start
  43.6 0.0 copy-start.1
  43.6 15.3 %attention.1 = (bf16[64,1,512,128]{3,2,1,0:T(8,128)(2,1)}, bf16[64,1,512,128]{3,2,1,0:T(8,128)(2,1)}, f32[64,5,128,128]{3,2,1,0:T(8,128)}, f32[8,8,5120]{2,1,0:T(8,128)S(1)}) custom-call(s32[64]{0:T(128)} %len_ref.1, bf16[64,5120]{1,0:T(8,128)(2,1)S(1)} %get-tuple-element.17.h2_ref, f32[3,64,128]{2,1,0:T(8,128)S(1)} %get-tuple-element.18.table_ref, ...), custom_call_target="tpu_custom_call" | custom-call | flops 1174405120 | bytes 33554432 | tf_op jit(solution)/shard_map/attention/pallas_call | solution.py:511
  58.9 0.0 copy-done
  58.9 0.0 copy-done.1
  58.9 20.6 %second_sum.1 = bf16[64,5120]{1,0:T(8,128)(2,1)S(1)} custom-call(f32[8,8,5120]{2,1,0:T(8,128)S(1)} %get-tuple-element.25.part_ref, f32[8,5120]{1,0:T(8,128)S(1)} %get-tuple-element.26.h2_ref, f32[2]{0:T(128)S(1)} %copy-done, f32[2]{0:T(128)S(1)} %copy-done.1), custom_call_target="tpu_custom_call" | custom-call | flops 99999997952 | bytes 100000000 | tf_op jit(solution)/shard_map/second_sum/pallas_call | solution.py:164
  79.6 0.8 %copy.22 = bf16[64,5120]{1,0:T(8,128)(2,1)} copy(bf16[64,5120]{1,0:T(8,128)(2,1)S(1)} %second_sum.1) | data formatting | bytes 1310720
Async XLA Ops:
  43.6 15.3 %copy-start = (f32[2]{0:T(128)S(1)}, f32[2]{0:T(128)}, u32[]{:S(2)}) copy-start(f32[2]{0:T(128)} %alpha_ref.1) | copy-start | bytes 28
  43.6 15.3 %copy-start.1 = (f32[2]{0:T(128)S(1)}, f32[2]{0:T(128)}, u32[]{:S(2)}) copy-start(f32[2]{0:T(128)} %beta_ref.1) | copy-start | bytes 28
